TPU v7x, 32 devices: a whole 2x2x4 slice. The times are simulated.
32 devices in a mesh: section: 4 (over y, x), dp: 8 (over z, core).
Axes of the slice: x: 2, y: 2, z: 4, core: 2. Of those that a mesh axis runs over, the one named last changes fastest.
Arguments:
- activations: bfloat16 [4, 8, 257, 1792], P('section', 'dp'), may hold values from -6 to 6
- saved: bfloat16 [4, 8, 257, 1792], P('section', 'dp'), may hold values from -6 to 6
- cotangents: bfloat16 [4, 8, 257, 1792], P('section', 'dp'), may hold values from -1.1953125 to 1.1953125
- projection: bfloat16 [4, 1792, 1792], P('section'), may hold values from -0.125 to 0.125
- section_gain: float32 [4, 1792], P('section'), may hold values from 0.5 to 1.5
- final_gain: float32 [1792], replicated, may hold values from 0.5 to 1.5
- head_weight: bfloat16 [1792, 1024], P('section'), may hold values from -0.125 to 0.125
- text_embed: bfloat16 [8, 1024], P('dp'), may hold values from -6 to 6
- labels: int32 [8], P('dp'), may hold values from 0 to 7, each once
Outputs:
- next_act: bfloat16 [4, 8, 257, 1792], P('section', 'dp')
- next_grad: bfloat16 [4, 8, 257, 1792], P('section', 'dp')
- mean_loss: float32 [4], P('section')
Inputs may be any that keep to these rules, and one draw needn't show every extreme that they name: labels holds each caption index once.
All inputs are finite; a program needn't handle non-finite values.
Results may differ from a plain program's by a relative error of at most 0.0039.
Values may be sent and summed in bfloat16 or wider, within the bound.
A program may use at most 64 MiB of HBM per device.

v0:
```python
import functools
import math

import jax
import jax.numpy as jnp
from jax import lax
from jax.experimental import pallas as pl
from jax.experimental.pallas import tpu as pltpu
from jax.sharding import PartitionSpec as P

epsilon = 1e-06
logit_scale = 100.0
MESH = pl.DeviceIdType.MESH


def exchange(slots, send, recv, axis, me, peers):
    def start(step, carry):
        peer = lax.rem(me + step, peers)
        pltpu.make_async_remote_copy(
            slots.at[me], slots.at[me], send.at[peer], recv.at[me], {axis: peer}, MESH
        ).start()
        return carry

    lax.fori_loop(1, peers, start, 0)


def arrived(slots, send, recv, axis, me, peers):
    def wait(step, carry):
        peer = lax.rem(me + step, peers)
        pltpu.make_async_remote_copy(
            slots.at[me], slots.at[peer], send.at[peer], recv.at[peer], {axis: peer}, MESH
        ).wait_recv()
        return carry

    lax.fori_loop(1, peers, wait, 0)


def sent(slots, send, recv, axis, me, peers):
    def wait(step, carry):
        peer = lax.rem(me + step, peers)
        pltpu.make_async_remote_copy(
            slots.at[me], slots.at[me], send.at[peer], recv.at[peer], {axis: peer}, MESH
        ).wait_send()
        return carry

    lax.fori_loop(1, peers, wait, 0)


def enter(sections, replicas):
    section, replica = lax.axis_index("section"), lax.axis_index("dp")
    barrier = pltpu.get_barrier_semaphore()

    def greet_section(step, carry):
        peer = lax.rem(section + step, sections)
        pl.semaphore_signal(barrier, inc=1, device_id={"section": peer}, device_id_type=MESH)
        return carry

    def greet_replica(step, carry):
        peer = lax.rem(replica + step, replicas)
        pl.semaphore_signal(barrier, inc=1, device_id={"dp": peer}, device_id_type=MESH)
        return carry

    lax.fori_loop(1, sections, greet_section, 0)
    lax.fori_loop(1, replicas, greet_replica, 0)
    pl.semaphore_wait(barrier, sections + replicas - 2)


def row_stats(values):
    width = values.shape[-1]
    centre = jnp.sum(values, axis=-1, keepdims=True) / width
    centred = values - centre
    variance = jnp.sum(centred * centred, axis=-1, keepdims=True) / width
    return centre, lax.rsqrt(variance + epsilon)


def step_kernel(
    sections,
    replicas,
    group,
    chunk,
    act_ref,
    saved_ref,
    cot_ref,
    weight_ref,
    head_ref,
    scale_ref,
    gain_ref,
    text_ref,
    label_ref,
    next_ref,
    grad_ref,
    row_ref,
    loss_ref,
    act,
    saved,
    cot,
    weight,
    normed,
    block,
    d_input,
    slope,
    pooled,
    heads,
    feats,
    columns,
    images,
    texts,
    d_rows,
    part_out,
    part_in,
    relay,
    load_sem,
    weight_sem,
    head_send,
    head_recv,
    fwd_send,
    fwd_recv,
    bwd_send,
    bwd_recv,
    feat_send,
    feat_recv,
    col_send,
    col_recv,
    image_send,
    image_recv,
    text_send,
    text_recv,
    part_send,
    part_recv,
    relay_recv,
    pass_send,
):
    section, replica = lax.axis_index("section"), lax.axis_index("dp")
    last = sections - 1
    tokens, width = act.shape
    rows, span = head_ref.shape
    shards = width // chunk
    slot = lax.rem(replica, group)
    first = replica - slot
    shard = span // group
    f32, bf16 = jnp.float32, jnp.bfloat16

    def cut(index):
        return pl.ds(pl.multiple_of(index * chunk, chunk), chunk)

    def weight_load(index):
        return pltpu.make_async_copy(
            weight_ref.at[:, cut(index)], weight.at[:, cut(index)], weight_sem.at[index]
        )

    load_act = pltpu.make_async_copy(act_ref, act, load_sem.at[0])
    load_saved = pltpu.make_async_copy(saved_ref, saved, load_sem.at[1])
    load_cot = pltpu.make_async_copy(cot_ref, cot, load_sem.at[2])
    load_act.start()
    for index in range(shards):
        weight_load(index).start()
    load_saved.start()
    load_cot.start()
    enter(sections, replicas)

    my_columns = pl.ds(pl.multiple_of(slot * shard, shard), shard)

    def head_rows(owner):
        return pl.ds(pl.multiple_of(owner * rows, rows), rows)

    def head_copy(owner):
        return pltpu.make_async_remote_copy(
            head_ref.at[:, my_columns],
            heads.at[head_rows(owner), :],
            head_send,
            head_recv.at[owner],
            {"section": last},
            MESH,
        )

    own_head = pltpu.make_async_copy(
        head_ref.at[:, my_columns], heads.at[head_rows(last), :], head_send
    )

    @pl.when(section < last)
    def _():
        head_copy(section).start()

    @pl.when(section == last)
    def _():
        own_head.start()
        text = text_ref[...].astype(f32)
        text_inv = lax.rsqrt(jnp.sum(text * text, axis=-1, keepdims=True) + epsilon)
        texts[replica, :, 0:span] = text * text_inv
        texts[replica, :, span:] = jnp.full((1, 128), label_ref[0]).astype(f32)
        exchange(texts, text_send, text_recv, "dp", replica, replicas)

    cutoff = tokens // 2 // 16 * 16
    halves = (pl.ds(0, cutoff), pl.ds(cutoff, tokens - cutoff))

    def move(source, target, send, recv, peer, half, index):
        part = (halves[half], cut(index))
        return pltpu.make_async_remote_copy(
            source.at[part],
            target.at[part],
            send.at[half, index],
            recv.at[half, index],
            {"section": peer},
            MESH,
        )

    def forward_copy(half, index):
        return move(block, next_ref, fwd_send, fwd_recv, section + 1, half, index)

    def backward_copy(half, index):
        return move(d_input, grad_ref, bwd_send, bwd_recv, section - 1, half, index)

    middle = sections // 2
    relays = sections >= 4
    forward_relay, backward_relay = middle + 1, middle - 2

    def forward_detour(index):
        return move(block, relay, fwd_send, relay_recv, forward_relay, 1, index)

    def backward_detour(index):
        return move(d_input, relay, bwd_send, relay_recv, backward_relay, 1, index)

    def forward_pass(index):
        return move(relay, next_ref, pass_send, fwd_recv, middle, 1, index)

    def backward_pass(index):
        return move(relay, grad_ref, pass_send, bwd_recv, middle - 1, 1, index)

    def send_piece(direct, detour, origin, index):
        direct(0, index).start()
        if not relays:
            direct(1, index).start()
            return

        @pl.when(section == origin)
        def _():
            detour(index).start()

        @pl.when(section != origin)
        def _():
            direct(1, index).start()

    def send_forward(index):
        send_piece(forward_copy, forward_detour, middle - 1, index)

    def send_backward(index):
        send_piece(backward_copy, backward_detour, middle, index)

    def relay_all(detour, onward):
        def go(index, carry):
            detour(index).wait_recv()
            onward(index).start()
            return carry

        lax.fori_loop(0, shards, go, 0)

    def forward_step(index, carry):
        @pl.when(section < last)
        def _():
            weight_load(index).wait()

        mixed = jnp.dot(normed[...], weight[:, cut(index)], preferred_element_type=f32)
        piece = (act[:, cut(index)].astype(f32) + mixed).astype(bf16)
        block[:, cut(index)] = piece
        pooled[:, cut(index)] = jnp.sum(piece.astype(f32), axis=0, keepdims=True) / tokens

        @pl.when(section < last)
        def _():
            send_forward(index)

        return carry

    def forward():
        load_act.wait()
        values = act[...].astype(f32)
        centre, inverse = row_stats(values)
        normed[...] = ((values - centre) * inverse * scale_ref[...]).astype(bf16)
        lax.fori_loop(0, shards, forward_step, 0)

    def backward():
        load_saved.wait()
        load_cot.wait()
        centre, inverse = row_stats(saved[...].astype(f32))

        def gradient_step(index, carry):
            sum_slope, sum_product = carry
            d_normed = lax.dot_general(
                cot[...],
                weight[cut(index), :],
                (((1,), (1,)), ((), ())),
                preferred_element_type=f32,
            )
            piece = d_normed * scale_ref[:, cut(index)]
            standard = (saved[:, cut(index)].astype(f32) - centre) * inverse
            slope[:, cut(index)] = piece
            return (
                sum_slope + jnp.sum(piece, axis=-1, keepdims=True),
                sum_product + jnp.sum(piece * standard, axis=-1, keepdims=True),
            )

        zero = jnp.zeros((tokens, 1), f32)
        sum_slope, sum_product = lax.fori_loop(0, shards, gradient_step, (zero, zero))
        mean_slope, mean_product = sum_slope / width, sum_product / width

        def emit_step(index, carry):
            standard = (saved[:, cut(index)].astype(f32) - centre) * inverse
            d_input[:, cut(index)] = (
                cot[:, cut(index)].astype(f32)
                + inverse * (slope[:, cut(index)] - mean_slope - standard * mean_product)
            ).astype(bf16)
            send_backward(index)
            return carry

        lax.fori_loop(0, shards, emit_step, 0)

    @pl.when(section == last)
    def _():
        for index in range(shards):
            weight_load(index).wait()
        backward()

    forward()

    @pl.when((section > 0) & (section < last))
    def _():
        backward()

    @pl.when(section == 0)
    def _():
        load_saved.wait()
        load_cot.wait()

    loss_ref[...] = jnp.zeros_like(loss_ref)
    row_ref[...] = jnp.zeros_like(row_ref)

    if relays:

        @pl.when(section == forward_relay)
        def _():
            relay_all(forward_detour, forward_pass)

        @pl.when(section == backward_relay)
        def _():
            relay_all(backward_detour, backward_pass)

    @pl.when(section == last)
    def _():
        mean_row = pooled[...]
        centre, pooled_inv = row_stats(mean_row)
        pooled_std = (mean_row - centre) * pooled_inv
        feats[slot] = (pooled_std * gain_ref[...].reshape(1, width)).astype(bf16).astype(f32)

        def in_group(make):
            def go(step, carry):
                peer = lax.rem(slot + step, group)
                make(peer)
                return carry

            lax.fori_loop(1, group, go, 0)

        def feat_copy(peer, source):
            return pltpu.make_async_remote_copy(
                feats.at[slot],
                feats.at[source],
                feat_send.at[peer],
                feat_recv.at[source],
                {"dp": first + peer},
                MESH,
            )

        def col_copy(peer, source):
            return pltpu.make_async_remote_copy(
                columns.at[slot],
                columns.at[source],
                col_send.at[peer],
                col_recv.at[source],
                {"dp": first + peer},
                MESH,
            )

        def part_copy(peer, source):
            return pltpu.make_async_remote_copy(
                part_out.at[peer],
                part_in.at[source],
                part_send.at[peer],
                part_recv.at[source],
                {"dp": first + peer},
                MESH,
            )

        in_group(lambda peer: feat_copy(peer, slot).start())
        own_head.wait()
        for owner in range(last):
            head_copy(owner).wait_recv()
        in_group(lambda peer: feat_copy(peer, peer).wait_recv())
        columns[slot] = jnp.dot(
            feats[:, 0, :].astype(bf16), heads[...], preferred_element_type=f32
        )
        in_group(lambda peer: col_copy(peer, slot).start())
        arrived(texts, text_send, text_recv, "dp", replica, replicas)
        all_text = texts[:, 0, 0:span]
        label_column = texts[:, 0, span : span + 1]
        column = lax.broadcasted_iota(jnp.int32, (replicas, replicas), 1)
        targets = jnp.where(label_column == column.astype(f32), 1.0, 0.0)
        in_group(lambda peer: col_copy(peer, peer).wait_recv())
        embedding = jnp.concatenate([columns[index] for index in range(group)], axis=1)
        image_inv = lax.rsqrt(jnp.sum(embedding * embedding, axis=-1, keepdims=True) + epsilon)
        image_unit = embedding * image_inv
        member = lax.broadcasted_iota(jnp.int32, (group, 1), 0)
        if replicas == group:
            all_image = image_unit
        else:
            images[replica] = jnp.sum(
                jnp.where(member == slot, image_unit, 0.0), axis=0, keepdims=True
            )
            exchange(images, image_send, image_recv, "dp", replica, replicas)
            arrived(images, image_send, image_recv, "dp", replica, replicas)
            all_image = images[:, 0, :]
        logits = logit_scale * lax.dot_general(
            all_image,
            all_text,
            (((1,), (1,)), ((), ())),
            precision=lax.Precision.HIGHEST,
            preferred_element_type=f32,
        )
        row_max = jnp.max(logits, axis=1, keepdims=True)
        row_lse = row_max + jnp.log(jnp.sum(jnp.exp(logits - row_max), axis=1, keepdims=True))
        col_max = jnp.max(logits, axis=0, keepdims=True)
        col_lse = col_max + jnp.log(jnp.sum(jnp.exp(logits - col_max), axis=0, keepdims=True))
        d_logits = 0.5 * (
            (jnp.exp(logits - row_lse) - targets) + (jnp.exp(logits - col_lse) - targets)
        )
        if replicas != group:
            pick_row = lax.broadcasted_iota(jnp.int32, (group, replicas), 0) + first
            pick_column = lax.broadcasted_iota(jnp.int32, (group, replicas), 1)
            d_logits = jnp.dot(
                jnp.where(pick_row == pick_column, 1.0, 0.0),
                d_logits,
                precision=lax.Precision.HIGHEST,
                preferred_element_type=f32,
            )
        d_image = logit_scale * jnp.dot(
            d_logits, all_text, precision=lax.Precision.HIGHEST, preferred_element_type=f32
        )
        along = jnp.sum(d_image * image_unit, axis=-1, keepdims=True)
        d_rows[...] = (d_image - image_unit * along) * image_inv
        partial = lax.dot_general(
            d_rows[:, my_columns].astype(bf16),
            heads[...],
            (((1,), (1,)), ((), ())),
            preferred_element_type=f32,
        )
        for index in range(group):
            part_out[index] = partial[index : index + 1, :]
        in_group(lambda peer: part_copy(peer, slot).start())
        part_in[slot] = jnp.sum(jnp.where(member == slot, partial, 0.0), axis=0, keepdims=True)
        picked = jnp.sum(logits * targets, axis=1, keepdims=True)
        col_picked = jnp.sum(col_lse * targets, axis=1, keepdims=True)
        loss = 0.5 * (row_lse - picked) + 0.5 * (col_picked - picked)
        loss_ref[...] = jnp.broadcast_to(
            jnp.sum(loss, axis=0, keepdims=True) / replicas, loss_ref.shape
        )
        in_group(lambda peer: part_copy(peer, peer).wait_recv())
        d_std = jnp.sum(part_in[...], axis=0) * gain_ref[...].reshape(1, width)
        d_pooled = pooled_inv * (
            d_std
            - jnp.sum(d_std, axis=-1, keepdims=True) / width
            - pooled_std * (jnp.sum(d_std * pooled_std, axis=-1, keepdims=True) / width)
        )
        row_ref[...] = d_pooled / tokens
        in_group(lambda peer: feat_copy(peer, peer).wait_send())
        in_group(lambda peer: col_copy(peer, peer).wait_send())
        in_group(lambda peer: part_copy(peer, peer).wait_send())
        sent(texts, text_send, text_recv, "dp", replica, replicas)
        if replicas != group:
            sent(images, image_send, image_recv, "dp", replica, replicas)

    @pl.when(section < last)
    def _():
        head_copy(section).wait_send()

    def drain(index, carry):
        for half in range(2):

            @pl.when(section < last)
            def _():
                forward_copy(half, index).wait_send()
                backward_copy(half, index).wait_recv()

            @pl.when(section > 0)
            def _():
                forward_copy(half, index).wait_recv()
                backward_copy(half, index).wait_send()

        if relays:

            @pl.when((section == forward_relay) | (section == backward_relay))
            def _():
                forward_pass(index).wait_send()

        return carry

    lax.fori_loop(0, shards, drain, 0)


def local(
    activations,
    saved,
    cotangents,
    projection,
    section_gain,
    final_gain,
    head_weight,
    text_embed,
    labels,
):
    sections, replicas = lax.axis_size("section"), lax.axis_size("dp")
    tokens, width = activations.shape[2:]
    rows, span = head_weight.shape
    group = math.gcd(replicas, span // 128)
    shard = span // group
    chunk = 256 if width % 256 == 0 else 128
    shards = width // chunk
    f32, bf16 = jnp.float32, jnp.bfloat16
    dma = pltpu.SemaphoreType.DMA
    vmem = pl.BlockSpec(memory_space=pltpu.VMEM)
    whole = pl.BlockSpec(memory_space=pl.ANY)
    next_raw, grad_raw, grad_row, loss_row = pl.pallas_call(
        functools.partial(step_kernel, sections, replicas, group, chunk),
        out_shape=(
            jax.ShapeDtypeStruct((tokens, width), bf16),
            jax.ShapeDtypeStruct((tokens, width), bf16),
            jax.ShapeDtypeStruct((1, width), f32),
            jax.ShapeDtypeStruct((1, 128), f32),
        ),
        in_specs=[whole] * 5 + [vmem] * 3 + [pl.BlockSpec(memory_space=pltpu.SMEM)],
        out_specs=(whole, whole, vmem, vmem),
        scratch_shapes=[
            pltpu.VMEM((tokens, width), bf16),
            pltpu.VMEM((tokens, width), bf16),
            pltpu.VMEM((tokens, width), bf16),
            pltpu.VMEM((width, width), bf16),
            pltpu.VMEM((tokens, width), bf16),
            pltpu.VMEM((tokens, width), bf16),
            pltpu.VMEM((tokens, width), bf16),
            pltpu.VMEM((tokens, width), f32),
            pltpu.VMEM((1, width), f32),
            pltpu.VMEM((sections * rows, shard), bf16),
            pltpu.VMEM((group, 1, width), f32),
            pltpu.VMEM((group, group, shard), f32),
            pltpu.VMEM((replicas, 1, span), f32),
            pltpu.VMEM((replicas, 1, span + 128), f32),
            pltpu.VMEM((group, span), f32),
            pltpu.VMEM((group, 1, width), f32),
            pltpu.VMEM((group, 1, width), f32),
            pltpu.VMEM((tokens, width), bf16),
            dma((3,)),
            dma((shards,)),
            dma,
            dma((sections,)),
            dma((2, shards)),
            dma((2, shards)),
            dma((2, shards)),
            dma((2, shards)),
            dma((group,)),
            dma((group,)),
            dma((group,)),
            dma((group,)),
            dma((replicas,)),
            dma((replicas,)),
            dma((replicas,)),
            dma((replicas,)),
            dma((group,)),
            dma((group,)),
            dma((2, shards)),
            dma((2, shards)),
        ],
        compiler_params=pltpu.CompilerParams(collective_id=0, has_side_effects=True),
        name="tower_step",
    )(
        activations[0, 0],
        saved[0, 0],
        cotangents[0, 0],
        projection[0],
        head_weight,
        section_gain,
        final_gain,
        text_embed,
        labels,
    )
    section = lax.axis_index("section")
    next_act = jnp.where(section == 0, jnp.zeros_like(next_raw), next_raw)
    next_grad = jnp.where(section == sections - 1, grad_row.astype(bf16), grad_raw)
    return (next_act[None, None], next_grad[None, None], loss_row[0, :1])


def solution(mesh):
    return jax.shard_map(
        local,
        mesh=mesh,
        in_specs=(
            P("section", "dp", None, None),
            P("section", "dp", None, None),
            P("section", "dp", None, None),
            P("section", None, None),
            P("section", None),
            P(),
            P("section", None),
            P("dp", None),
            P("dp"),
        ),
        out_specs=(P("section", "dp", None, None), P("section", "dp", None, None), P("section")),
        check_vma=False,
    )
```

profile of v0, /device:TPU:28, one launch (start us, length us, event | category | flops | bytes accessed | tf_op | source)
XLA Modules:
  0.0 51.0 jit_solution(4552040773150889118)
XLA Ops:
  1.3 44.4 %tower_step.1 = (bf16[257,1792]{1,0:T(8,128)(2,1)}, bf16[257,1792]{1,0:T(8,128)(2,1)}, f32[1,1792]{1,0:T(1,128)}, f32[1,128]{1,0:T(1,128)}) custom-call(bf16[257,1792]{1,0:T(8,128)(2,1)} %bitcast.11, bf16[257,1792]{1,0:T(8,128)(2,1)} %bitcast.12, bf16[257,1792]{1,0:T(8,128)(2,1)} %bitcast.13, bf16[1792,1792]{1,0:T(8,128)(2,1)} %bitcast.10, ...), custom_call_target="tpu_custom_call" | custom-call | tf_op jit(solution)/shard_map/tower_step/pallas_call | solution.py:528
  45.7 0.7 %convert_reduce_fusion = bf16[1792]{0:T(1024)(128)(2,1)S(1)} fusion(f32[1,1792]{1,0:T(1,128)} %get-tuple-element.8), kind=kLoop, calls=%fused_computation.2 | loop fusion | flops 1792 | bytes 10752 | tf_op jit(solution)/shard_map/convert_element_type | solution.py:593
  46.5 2.9 %select_bitcast_fusion = (bf16[1,1,257,1792]{3,2,1,0:T(8,128)(2,1)}, bf16[1,1,257,1792]{3,2,1,0:T(8,128)(2,1)}) fusion(bf16[257,1792]{1,0:T(8,128)(2,1)} %get-tuple-element.9, pred[]{:T(512)S(6)} %eq.7, bf16[1792]{0:T(1024)(128)(2,1)S(1)} %convert_reduce_fusion, bf16[257,1792]{1,0:T(8,128)(2,1)} %get-tuple-element.7, pred[]{:T(512)S(6)} %eq.6), kind=kLoop, calls=%fused_computation | loop fusion | flops 921088 | bytes 3687938 | tf_op jit(solution)/shard_map/broadcast_in_dim | solution.py:594
where the time goes:
time: 51.5 us; the launch traced here: 51 us
  Pallas kernels  44.4 us (86%)
  other arithmetic  3.58 us (7%)
  between operations  2.97 us (6%)
    pallas_call x1, Pallas kernels, local(): pl.pallas_call(functools.partial(step_kernel, sections, replicas, group,...  44.4 us
    broadcast_in_dim x1, other arithmetic, local(): return (next_act[None, None], next_grad[None, None], loss_row[0, :1])  2.86 us

commit v1 on v0

v1 whole, which is shorter than its diff:
```python
import functools
import math

import jax
import jax.numpy as jnp
from jax import lax
from jax.experimental import pallas as pl
from jax.experimental.pallas import tpu as pltpu
from jax.sharding import PartitionSpec as P

epsilon = 1e-06
logit_scale = 100.0
MESH = pl.DeviceIdType.MESH
forward_share = 0.56
backward_share = 0.5


def row_stats(values):
    width = values.shape[-1]
    centre = jnp.sum(values, axis=-1, keepdims=True) / width
    centred = values - centre
    variance = jnp.sum(centred * centred, axis=-1, keepdims=True) / width
    return centre, lax.rsqrt(variance + epsilon)


def step_kernel(
    sections,
    replicas,
    group,
    unit,
    act_ref,
    saved_ref,
    cot_ref,
    weight_ref,
    head_ref,
    scale_ref,
    gain_ref,
    text_ref,
    label_ref,
    next_ref,
    grad_ref,
    loss_ref,
    act,
    saved,
    cot,
    weight,
    normed,
    block,
    d_input,
    slope,
    sum_slope,
    sum_product,
    pooled,
    scale,
    gain,
    text,
    label,
    heads,
    feats,
    columns,
    images,
    texts,
    d_rows,
    part_out,
    part_in,
    relay,
    load_sem,
    weight_sem,
    head_sem,
    bulk_send,
    bulk_recv,
    relay_recv,
    small_send,
    small_recv,
):
    section, replica = lax.axis_index("section"), lax.axis_index("dp")
    last = sections - 1
    tokens, width = act.shape
    rows, span = head_ref.shape
    shards = width // unit
    pairs = (shards - 1) // 2
    slot = lax.rem(replica, group)
    first = replica - slot
    shard = span // group
    f32, bf16 = jnp.float32, jnp.bfloat16
    wide = 2 * unit
    lead = [(0, unit)]
    tail = [(unit + pairs * wide, width - unit - pairs * wide)] if (shards - 1) % 2 else []
    n_chunks = 1 + pairs + len(tail)

    def cut(start, size):
        return pl.ds(start if isinstance(start, int) else pl.multiple_of(start, unit), size)

    def each_chunk(step):
        step(0, 0, unit)
        if pairs:

            def go(index, carry):
                step(index + 1, unit + index * wide, wide)
                return carry

            lax.fori_loop(0, pairs, go, 0)
        for start, size in tail:
            step(n_chunks - 1, start, size)

    static_chunks = (
        lead + [(unit + index * wide, wide) for index in range(pairs)] + tail
    )

    def column_load(index, start, size):
        part = cut(start, size)
        return pltpu.make_async_copy(
            weight_ref.at[:, part], weight.at[:, part], weight_sem.at[index]
        )

    def row_load(index, start, size):
        part = cut(start, size)
        return pltpu.make_async_copy(
            weight_ref.at[part, :], weight.at[part, :], weight_sem.at[index]
        )

    load_act = pltpu.make_async_copy(act_ref, act, load_sem.at[0])
    load_saved = pltpu.make_async_copy(saved_ref, saved, load_sem.at[1])
    load_cot = pltpu.make_async_copy(cot_ref, cot, load_sem.at[2])
    load_scale = pltpu.make_async_copy(scale_ref, scale, load_sem.at[3])
    load_gain = pltpu.make_async_copy(gain_ref, gain, load_sem.at[4])
    load_text = pltpu.make_async_copy(text_ref, text, load_sem.at[5])
    load_label = pltpu.make_async_copy(label_ref, label, load_sem.at[6])

    barrier = pltpu.get_barrier_semaphore()

    def greet(axis, me, peers):
        def go(step, carry):
            peer = lax.rem(me + step, peers)
            pl.semaphore_signal(barrier, inc=1, device_id={axis: peer}, device_id_type=MESH)
            return carry

        lax.fori_loop(1, peers, go, 0)

    greet("section", section, sections)
    load_scale.start()

    @pl.when(section < last)
    def _():
        load_act.start()
        for index, (start, size) in enumerate(static_chunks):
            column_load(index, start, size).start()

        @pl.when(section > 0)
        def _():
            load_saved.start()
            load_cot.start()

    @pl.when(section == last)
    def _():
        greet("dp", replica, replicas)
        load_cot.start()
        for index, (start, size) in enumerate(static_chunks):
            row_load(index, start, size).start()
            if index == 0:
                load_saved.start()
        load_act.start()
        load_text.start()
        load_label.start()
        load_gain.start()

    my_columns = pl.ds(pl.multiple_of(slot * shard, shard), shard)
    away = pl.ds(0, last * rows)

    def head_copy():
        return pltpu.make_async_remote_copy(
            head_ref.at[:, my_columns],
            heads.at[pl.ds(pl.multiple_of(section * rows, rows), rows), :],
            head_sem.at[0],
            head_sem.at[1],
            {"section": last},
            MESH,
        )

    head_arrival = pltpu.make_async_remote_copy(
        heads.at[away, :], heads.at[away, :], head_sem.at[0], head_sem.at[1], {"section": 0}, MESH
    )
    own_head = pltpu.make_async_copy(
        head_ref.at[:, my_columns], heads.at[pl.ds(last * rows, rows), :], head_sem.at[0]
    )

    everything = (slice(None), slice(None))
    forward_send, backward_send, pass_send = bulk_send.at[0], bulk_send.at[1], bulk_send.at[2]
    forward_recv, backward_recv = bulk_recv.at[0], bulk_recv.at[1]

    def move(source, target, send, recv, peer, part):
        return pltpu.make_async_remote_copy(
            source.at[part], target.at[part], send, recv, {"section": peer}, MESH
        )

    def forward_copy(part):
        return move(block, next_ref, forward_send, forward_recv, section + 1, part)

    def backward_copy(part):
        return move(d_input, grad_ref, backward_send, backward_recv, section - 1, part)

    middle = sections // 2
    relays = sections >= 4
    forward_relay, backward_relay = middle + 1, middle - 2

    def rows_at(share):
        edge = int(tokens * share) // 16 * 16
        return pl.ds(0, edge), pl.ds(edge, tokens - edge)

    forward_near, forward_far = rows_at(forward_share)
    backward_near, backward_far = rows_at(backward_share)

    def forward_detour(index, columns_part):
        return move(
            block,
            relay,
            forward_send,
            relay_recv.at[index],
            forward_relay,
            (forward_far, columns_part),
        )

    def backward_detour(index, columns_part):
        return move(
            d_input,
            relay,
            backward_send,
            relay_recv.at[index],
            backward_relay,
            (backward_far, columns_part),
        )

    def forward_pass(columns_part):
        return move(
            relay, next_ref, pass_send, forward_recv, middle, (forward_far, columns_part)
        )

    def backward_pass(columns_part):
        return move(
            relay, grad_ref, pass_send, backward_recv, middle - 1, (backward_far, columns_part)
        )

    def send_piece(direct, detour, origin, near, index, columns_part):
        if not relays:
            direct((slice(None), columns_part)).start()
            return

        @pl.when(section == origin)
        def _():
            direct((near, columns_part)).start()
            detour(index, columns_part).start()

        @pl.when(section != origin)
        def _():
            direct((slice(None), columns_part)).start()

    def forward():
        load_act.wait()
        values = act[...].astype(f32)
        centre, inverse = row_stats(values)
        normed[...] = ((values - centre) * inverse * scale[...]).astype(bf16)

        def step(index, start, size):
            part = cut(start, size)

            @pl.when(section < last)
            def _():
                column_load(index, start, size).wait()

            mixed = jnp.dot(normed[...], weight[:, part], preferred_element_type=f32)
            piece = (act[:, part].astype(f32) + mixed).astype(bf16)
            block[:, part] = piece
            pooled[:, part] = jnp.sum(piece.astype(f32), axis=0, keepdims=True) / tokens

            @pl.when(section < last)
            def _():
                send_piece(forward_copy, forward_detour, middle - 1, forward_near, index, part)

        each_chunk(step)

    def folded(values):
        total = values[:, 0:128]
        for start in range(128, values.shape[-1], 128):
            total = total + values[:, start : start + 128]
        return total

    def backward(wait_rows, before_send):
        load_saved.wait()
        centre, inverse = row_stats(saved[...].astype(f32))
        load_cot.wait()
        sum_slope[...] = jnp.zeros_like(sum_slope)
        sum_product[...] = jnp.zeros_like(sum_product)

        def step(index, start, size):
            part = cut(start, size)
            if wait_rows:
                row_load(index, start, size).wait()
            d_normed = lax.dot_general(
                cot[...],
                weight[part, :],
                (((1,), (1,)), ((), ())),
                preferred_element_type=f32,
            )
            piece = d_normed * scale[:, part]
            slope[:, part] = piece
            sum_slope[...] += folded(piece)
            sum_product[...] += folded(piece * (saved[:, part].astype(f32) - centre))

        each_chunk(step)
        mean_slope = jnp.sum(sum_slope[...], axis=-1, keepdims=True) / width
        mean_product = inverse * (jnp.sum(sum_product[...], axis=-1, keepdims=True) / width)
        offset = inverse * mean_slope
        factor = inverse * inverse * mean_product
        before_send()

        def emit(index, carry):
            part = cut(index * unit, unit)
            d_input[:, part] = (
                cot[:, part].astype(f32)
                + (
                    (inverse * slope[:, part] - offset)
                    - (saved[:, part].astype(f32) - centre) * factor
                )
            ).astype(bf16)
            send_piece(backward_copy, backward_detour, middle, backward_near, index, part)
            return carry

        lax.fori_loop(0, shards, emit, 0)

    def exchange(slots, pair, axis, me, base, peers):
        def go(step, carry):
            peer = lax.rem(me + step, peers)
            pltpu.make_async_remote_copy(
                slots.at[me],
                slots.at[me],
                small_send.at[pair],
                small_recv.at[pair],
                {axis: base + peer},
                MESH,
            ).start()
            return carry

        lax.fori_loop(1, peers, go, 0)

    def settle(slots, pair, peers):
        others = slots.at[pl.ds(0, peers - 1)]
        return pltpu.make_async_remote_copy(
            others, others, small_send.at[pair], small_recv.at[pair], {"dp": 0}, MESH
        )

    @pl.when(section == last)
    def _():
        load_scale.wait()

        def before_send():
            pl.semaphore_wait(barrier, sections + replicas - 2)
            own_head.start()
            load_text.wait()
            load_label.wait()
            values = text[...].astype(f32)
            text_inv = lax.rsqrt(jnp.sum(values * values, axis=-1, keepdims=True) + epsilon)
            texts[replica, :, 0:span] = values * text_inv
            texts[replica, :, span:] = jnp.full((1, 128), label[0]).astype(f32)
            exchange(texts, 0, "dp", replica, 0, replicas)

        backward(True, before_send)

    @pl.when(section < last)
    def _():
        pl.semaphore_wait(barrier, sections - 1)
        head_copy().start()
        load_scale.wait()

    forward()

    @pl.when((section > 0) & (section < last))
    def _():
        backward(False, lambda: None)

    @pl.when(section == 0)
    def _():
        next_ref[...] = jnp.zeros_like(next_ref)

    @pl.when(section < last)
    def _():
        loss_ref[0] = jnp.float32(0)

    def forward_relays():
        def go(index, start, size):
            part = cut(start, size)
            forward_detour(index, part).wait_recv()
            forward_pass(part).start()

        each_chunk(go)

    def backward_relays():
        def go(index, carry):
            part = cut(index * unit, unit)
            backward_detour(index, part).wait_recv()
            backward_pass(part).start()
            return carry

        lax.fori_loop(0, shards, go, 0)

    if relays:

        @pl.when(section == backward_relay)
        def _():
            backward_relays()

        if forward_relay != last:

            @pl.when(section == forward_relay)
            def _():
                forward_relays()

    @pl.when(section == last)
    def _():
        load_gain.wait()
        final_gain = gain[...].reshape(1, width)
        mean_row = pooled[...]
        centre, pooled_inv = row_stats(mean_row)
        pooled_std = (mean_row - centre) * pooled_inv
        feats[slot] = (pooled_std * final_gain).astype(bf16).astype(f32)
        if group > 1:
            exchange(feats, 1, "dp", slot, first, group)
        own_head.wait()
        head_arrival.wait_recv()
        if group > 1:
            settle(feats, 1, group).wait_recv()
        columns[slot] = jnp.dot(
            feats[:, 0, :].astype(bf16), heads[...], preferred_element_type=f32
        )
        if group > 1:
            exchange(columns, 2, "dp", slot, first, group)
        settle(texts, 0, replicas).wait_recv()
        all_text = texts[:, 0, 0:span]
        label_column = texts[:, 0, span : span + 1]
        column = lax.broadcasted_iota(jnp.int32, (replicas, replicas), 1)
        targets = jnp.where(label_column == column.astype(f32), 1.0, 0.0)
        if group > 1:
            settle(columns, 2, group).wait_recv()
        if relays and forward_relay == last:
            forward_relays()
        embedding = jnp.concatenate([columns[index] for index in range(group)], axis=1)
        image_inv = lax.rsqrt(jnp.sum(embedding * embedding, axis=-1, keepdims=True) + epsilon)
        image_unit = embedding * image_inv
        member = lax.broadcasted_iota(jnp.int32, (group, 1), 0)
        if replicas == group:
            all_image = image_unit
        else:
            images[replica] = jnp.sum(
                jnp.where(member == slot, image_unit, 0.0), axis=0, keepdims=True
            )
            exchange(images, 3, "dp", replica, 0, replicas)
            settle(images, 3, replicas).wait_recv()
            all_image = images[:, 0, :]
        logits = logit_scale * lax.dot_general(
            all_image,
            all_text,
            (((1,), (1,)), ((), ())),
            precision=lax.Precision.HIGHEST,
            preferred_element_type=f32,
        )
        row_max = jnp.max(logits, axis=1, keepdims=True)
        row_lse = row_max + jnp.log(jnp.sum(jnp.exp(logits - row_max), axis=1, keepdims=True))
        col_max = jnp.max(logits, axis=0, keepdims=True)
        col_lse = col_max + jnp.log(jnp.sum(jnp.exp(logits - col_max), axis=0, keepdims=True))
        d_logits = 0.5 * (
            (jnp.exp(logits - row_lse) - targets) + (jnp.exp(logits - col_lse) - targets)
        )
        if replicas != group:
            pick_row = lax.broadcasted_iota(jnp.int32, (group, replicas), 0) + first
            pick_column = lax.broadcasted_iota(jnp.int32, (group, replicas), 1)
            d_logits = jnp.dot(
                jnp.where(pick_row == pick_column, 1.0, 0.0),
                d_logits,
                precision=lax.Precision.HIGHEST,
                preferred_element_type=f32,
            )
        d_image = logit_scale * jnp.dot(
            d_logits, all_text, precision=lax.Precision.HIGHEST, preferred_element_type=f32
        )
        along = jnp.sum(d_image * image_unit, axis=-1, keepdims=True)
        d_rows[...] = (d_image - image_unit * along) * image_inv
        partial = lax.dot_general(
            d_rows[:, my_columns].astype(bf16),
            heads[...],
            (((1,), (1,)), ((), ())),
            preferred_element_type=f32,
        )
        for index in range(group):
            part_out[index] = partial[index : index + 1, :]

        def send_part(step, carry):
            peer = lax.rem(slot + step, group)
            pltpu.make_async_remote_copy(
                part_out.at[peer],
                part_in.at[slot],
                small_send.at[4],
                small_recv.at[4],
                {"dp": first + peer},
                MESH,
            ).start()
            return carry

        lax.fori_loop(1, group, send_part, 0)
        part_in[slot] = jnp.sum(jnp.where(member == slot, partial, 0.0), axis=0, keepdims=True)
        picked = jnp.sum(logits * targets, axis=1, keepdims=True)
        col_picked = jnp.sum(col_lse * targets, axis=1, keepdims=True)
        loss = 0.5 * (row_lse - picked) + 0.5 * (col_picked - picked)
        loss_ref[0] = jnp.sum(loss) / replicas
        if group > 1:
            settle(part_in, 4, group).wait_recv()
        d_std = jnp.sum(part_in[...], axis=0) * final_gain
        d_pooled = pooled_inv * (
            d_std
            - jnp.sum(d_std, axis=-1, keepdims=True) / width
            - pooled_std * (jnp.sum(d_std * pooled_std, axis=-1, keepdims=True) / width)
        )
        grad_ref[...] = jnp.broadcast_to(d_pooled / tokens, (tokens, width)).astype(bf16)
        settle(texts, 0, replicas).wait_send()
        if group > 1:
            settle(feats, 1, group).wait_send()
            settle(columns, 2, group).wait_send()
            settle(part_out, 4, group).wait_send()
        if replicas != group:
            settle(images, 3, replicas).wait_send()

    @pl.when(section < last)
    def _():
        head_copy().wait_send()
        forward_copy(everything).wait_send()
        backward_copy(everything).wait_recv()

    @pl.when(section > 0)
    def _():
        backward_copy(everything).wait_send()
        forward_copy(everything).wait_recv()

    if relays:

        @pl.when(section == forward_relay)
        def _():
            forward_pass(slice(None)).wait_send()

        @pl.when(section == backward_relay)
        def _():
            backward_pass(slice(None)).wait_send()


def local(
    activations,
    saved,
    cotangents,
    projection,
    section_gain,
    final_gain,
    head_weight,
    text_embed,
    labels,
):
    sections, replicas = lax.axis_size("section"), lax.axis_size("dp")
    tokens, width = activations.shape[2:]
    rows, span = head_weight.shape
    group = math.gcd(replicas, span // 128)
    shard = span // group
    unit = 256 if width % 256 == 0 else 128
    shards = width // unit
    chunks = 1 + (shards - 1) // 2 + (shards - 1) % 2
    f32, bf16 = jnp.float32, jnp.bfloat16
    dma = pltpu.SemaphoreType.DMA
    vmem = pl.BlockSpec(memory_space=pltpu.VMEM)
    whole = pl.BlockSpec(memory_space=pl.ANY)
    big = pltpu.VMEM((tokens, width), bf16)
    next_raw, grad_raw, loss = pl.pallas_call(
        functools.partial(step_kernel, sections, replicas, group, unit),
        out_shape=(big, big, jax.ShapeDtypeStruct((1,), f32)),
        in_specs=[whole] * 9,
        out_specs=(vmem, vmem, pl.BlockSpec(memory_space=pltpu.SMEM)),
        scratch_shapes=[
            big,
            big,
            big,
            pltpu.VMEM((width, width), bf16),
            big,
            big,
            big,
            pltpu.VMEM((tokens, width), f32),
            pltpu.VMEM((tokens, 128), f32),
            pltpu.VMEM((tokens, 128), f32),
            pltpu.VMEM((1, width), f32),
            pltpu.VMEM((1, width), f32),
            pltpu.VMEM((width,), f32),
            pltpu.VMEM((1, span), bf16),
            pltpu.SMEM((1,), jnp.int32),
            pltpu.VMEM((sections * rows, shard), bf16),
            pltpu.VMEM((group, 1, width), f32),
            pltpu.VMEM((group, group, shard), f32),
            pltpu.VMEM((replicas, 1, span), f32),
            pltpu.VMEM((replicas, 1, span + 128), f32),
            pltpu.VMEM((group, span), f32),
            pltpu.VMEM((group, 1, width), f32),
            pltpu.VMEM((group, 1, width), f32),
            big,
            dma((7,)),
            dma((chunks,)),
            dma((2,)),
            dma((3,)),
            dma((2,)),
            dma((shards,)),
            dma((5,)),
            dma((5,)),
        ],
        compiler_params=pltpu.CompilerParams(
            collective_id=0, has_side_effects=True, vmem_limit_bytes=40 * 1024 * 1024
        ),
        name="tower_step",
    )(
        activations[0, 0],
        saved[0, 0],
        cotangents[0, 0],
        projection[0],
        head_weight,
        section_gain,
        final_gain,
        text_embed,
        labels,
    )
    return (next_raw[None, None], grad_raw[None, None], loss)


def solution(mesh):
    return jax.shard_map(
        local,
        mesh=mesh,
        in_specs=(
            P("section", "dp", None, None),
            P("section", "dp", None, None),
            P("section", "dp", None, None),
            P("section", None, None),
            P("section", None),
            P(),
            P("section", None),
            P("dp", None),
            P("dp"),
        ),
        out_specs=(P("section", "dp", None, None), P("section", "dp", None, None), P("section")),
        check_vma=False,
    )
```

time: 51.5 us -> 53.8 us (1.045)
  local copies, waits for them, and re-layouts: 0 us -> 11.5 us
  Pallas kernels: 44.4 us -> 38.7 us
  other arithmetic: 3.58 us -> 0 us
    unnamed x0 -> x18, local copies, waits for them, and re-layouts: none -> 11.5 us
    pallas_call x1, Pallas kernels: 44.4 us -> 38.7 us  [local(): pl.pallas_call(functools.partial(step_kernel, sections, replicas, group,...]
    broadcast_in_dim x1 -> x0, other arithmetic: 2.86 us -> none  [local(): return (next_act[None, None], next_grad[None, None], loss_row[0, :1])]
    convert_element_type x1 -> x0, other arithmetic: 0.72 us -> none  [local(): grad_row.astype(bf16)]
where the time goes in v1:
time: 53.8 us; the launch traced here: 53.3 us
  Pallas kernels  38.7 us (72%)
  local copies, waits for them, and re-layouts  11.5 us (21%)
  between operations  3.12 us (6%)
    pallas_call x1, Pallas kernels, local(): pl.pallas_call(functools.partial(step_kernel, sections, replicas, group,...  38.7 us
    unnamed x18, local copies, waits for them, and re-layouts  11.5 us

profile of v1, /device:TPU:28, one launch (start us, length us, event | category | flops | bytes accessed | tf_op | source)
XLA Modules:
  0.0 53.3 jit_solution(15581527168611889144)
XLA Ops:
  1.3 0.0 copy-start
  1.3 2.8 %copy-done = bf16[1,1792,1792]{2,1,0:T(8,128)(2,1)S(1)} copy-done((bf16[1,1792,1792]{2,1,0:T(8,128)(2,1)S(1)}, bf16[1,1792,1792]{2,1,0:T(8,128)(2,1)}, u32[]{:S(2)}) %copy-start) | copy-done | bytes 6422552
  4.1 0.0 copy-start.1
  4.1 1.2 %copy-done.1 = bf16[1,1,257,1792]{3,2,1,0:T(8,128)(2,1)S(1)} copy-done((bf16[1,1,257,1792]{3,2,1,0:T(8,128)(2,1)S(1)}, bf16[1,1,257,1792]{3,2,1,0:T(8,128)(2,1)}, u32[]{:S(2)}) %copy-start.1) | copy-done | bytes 921112
  5.3 0.0 copy-start.2
  5.3 1.2 %copy-done.2 = bf16[1,1,257,1792]{3,2,1,0:T(8,128)(2,1)S(1)} copy-done((bf16[1,1,257,1792]{3,2,1,0:T(8,128)(2,1)S(1)}, bf16[1,1,257,1792]{3,2,1,0:T(8,128)(2,1)}, u32[]{:S(2)}) %copy-start.2) | copy-done | bytes 921112
  6.5 0.0 copy-start.3
  6.5 1.2 %copy-done.3 = bf16[1,1,257,1792]{3,2,1,0:T(8,128)(2,1)S(1)} copy-done((bf16[1,1,257,1792]{3,2,1,0:T(8,128)(2,1)S(1)}, bf16[1,1,257,1792]{3,2,1,0:T(8,128)(2,1)}, u32[]{:S(2)}) %copy-start.3) | copy-done | bytes 921112
  7.7 0.0 copy-start.4
  7.7 1.2 %copy-done.4 = bf16[448,1024]{1,0:T(8,128)(2,1)S(1)} copy-done((bf16[448,1024]{1,0:T(8,128)(2,1)S(1)}, bf16[448,1024]{1,0:T(8,128)(2,1)}, u32[]{:S(2)}) %copy-start.4) | copy-done | bytes 917528
  8.9 0.0 copy-start.5
  8.9 0.7 %copy-done.5 = f32[1792]{0:T(1024)S(1)} copy-done((f32[1792]{0:T(1024)S(1)}, f32[1792]{0:T(1024)}, u32[]{:S(2)}) %copy-start.5) | copy-done | bytes 7192
  9.5 0.0 copy-start.6
  9.6 0.7 %copy-done.6 = f32[1,1792]{1,0:T(1,128)S(1)} copy-done((f32[1,1792]{1,0:T(1,128)S(1)}, f32[1,1792]{1,0:T(1,128)}, u32[]{:S(2)}) %copy-start.6) | copy-done | bytes 7192
  10.2 0.0 copy-start.7
  10.2 0.7 %copy-done.7 = bf16[1,1024]{1,0:T(2,128)(2,1)S(1)} copy-done((bf16[1,1024]{1,0:T(2,128)(2,1)S(1)}, bf16[1,1024]{1,0:T(2,128)(2,1)}, u32[]{:S(2)}) %copy-start.7) | copy-done | bytes 2072
  10.9 38.7 %tower_step.1 = (bf16[257,1792]{1,0:T(8,128)(2,1)S(1)}, bf16[257,1792]{1,0:T(8,128)(2,1)S(1)}, f32[1]{0:T(128)}) custom-call(bf16[257,1792]{1,0:T(8,128)(2,1)S(1)} %bitcast.9, bf16[257,1792]{1,0:T(8,128)(2,1)S(1)} %bitcast.10, bf16[257,1792]{1,0:T(8,128)(2,1)S(1)} %bitcast.11, bf16[1792,1792]{1,0:T(8,128)(2,1)S(1)} %bitcast.8, ...), custom_call_target="tpu_custom_call" | custom-call | tf_op jit(solution)/shard_map/tower_step/pallas_call | solution.py:576
  49.6 0.9 %copy.15 = bf16[1,1,257,1792]{3,2,1,0:T(8,128)(2,1)} copy(bf16[1,1,257,1792]{3,2,1,0:T(8,128)(2,1)S(1)} %bitcast.7) | data formatting | bytes 1842176
  50.6 0.9 %copy.16 = bf16[1,1,257,1792]{3,2,1,0:T(8,128)(2,1)} copy(bf16[1,1,257,1792]{3,2,1,0:T(8,128)(2,1)S(1)} %bitcast.6) | data formatting | bytes 1842176
Async XLA Ops:
  1.3 2.8 %copy-start = (bf16[1,1792,1792]{2,1,0:T(8,128)(2,1)S(1)}, bf16[1,1792,1792]{2,1,0:T(8,128)(2,1)}, u32[]{:S(2)}) copy-start(bf16[1,1792,1792]{2,1,0:T(8,128)(2,1)} %param.12) | copy-start | bytes 19267588
  4.1 1.2 %copy-start.1 = (bf16[1,1,257,1792]{3,2,1,0:T(8,128)(2,1)S(1)}, bf16[1,1,257,1792]{3,2,1,0:T(8,128)(2,1)}, u32[]{:S(2)}) copy-start(bf16[1,1,257,1792]{3,2,1,0:T(8,128)(2,1)} %param.9) | copy-start | bytes 2763268
  5.3 1.2 %copy-start.2 = (bf16[1,1,257,1792]{3,2,1,0:T(8,128)(2,1)S(1)}, bf16[1,1,257,1792]{3,2,1,0:T(8,128)(2,1)}, u32[]{:S(2)}) copy-start(bf16[1,1,257,1792]{3,2,1,0:T(8,128)(2,1)} %param.10) | copy-start | bytes 2763268
  6.5 1.2 %copy-start.3 = (bf16[1,1,257,1792]{3,2,1,0:T(8,128)(2,1)S(1)}, bf16[1,1,257,1792]{3,2,1,0:T(8,128)(2,1)}, u32[]{:S(2)}) copy-start(bf16[1,1,257,1792]{3,2,1,0:T(8,128)(2,1)} %param.11) | copy-start | bytes 2763268
  7.7 1.2 %copy-start.4 = (bf16[448,1024]{1,0:T(8,128)(2,1)S(1)}, bf16[448,1024]{1,0:T(8,128)(2,1)}, u32[]{:S(2)}) copy-start(bf16[448,1024]{1,0:T(8,128)(2,1)} %head_ref.1) | copy-start | bytes 2752516
  8.9 0.7 %copy-start.5 = (f32[1792]{0:T(1024)S(1)}, f32[1792]{0:T(1024)}, u32[]{:S(2)}) copy-start(f32[1792]{0:T(1024)} %gain_ref.1) | copy-start | bytes 21508
  9.5 0.7 %copy-start.6 = (f32[1,1792]{1,0:T(1,128)S(1)}, f32[1,1792]{1,0:T(1,128)}, u32[]{:S(2)}) copy-start(f32[1,1792]{1,0:T(1,128)} %scale_ref.1) | copy-start | bytes 21508
  10.2 0.7 %copy-start.7 = (bf16[1,1024]{1,0:T(2,128)(2,1)S(1)}, bf16[1,1024]{1,0:T(2,128)(2,1)}, u32[]{:S(2)}) copy-start(bf16[1,1024]{1,0:T(2,128)(2,1)} %text_ref.1) | copy-start | bytes 6148

commit v2 on v1

--- a/solution.py
+++ b/solution.py
@@ -54,7 +54,6 @@
     scale,
     gain,
     text,
-    label,
     heads,
     feats,
     columns,
@@ -125,7 +124,6 @@
     load_scale = pltpu.make_async_copy(scale_ref, scale, load_sem.at[3])
     load_gain = pltpu.make_async_copy(gain_ref, gain, load_sem.at[4])
     load_text = pltpu.make_async_copy(text_ref, text, load_sem.at[5])
-    load_label = pltpu.make_async_copy(label_ref, label, load_sem.at[6])
 
     barrier = pltpu.get_barrier_semaphore()
 
@@ -161,7 +159,6 @@
                 load_saved.start()
         load_act.start()
         load_text.start()
-        load_label.start()
         load_gain.start()
 
     my_columns = pl.ds(pl.multiple_of(slot * shard, shard), shard)
@@ -356,11 +353,10 @@
             pl.semaphore_wait(barrier, sections + replicas - 2)
             own_head.start()
             load_text.wait()
-            load_label.wait()
             values = text[...].astype(f32)
             text_inv = lax.rsqrt(jnp.sum(values * values, axis=-1, keepdims=True) + epsilon)
             texts[replica, :, 0:span] = values * text_inv
-            texts[replica, :, span:] = jnp.full((1, 128), label[0]).astype(f32)
+            texts[replica, :, span:] = jnp.full((1, 128), label_ref[0]).astype(f32)
             exchange(texts, 0, "dp", replica, 0, replicas)
 
         backward(True, before_send)
@@ -383,7 +379,7 @@
 
     @pl.when(section < last)
     def _():
-        loss_ref[0] = jnp.float32(0)
+        loss_ref[...] = jnp.zeros_like(loss_ref)
 
     def forward_relays():
         def go(index, start, size):
@@ -509,7 +505,9 @@
         picked = jnp.sum(logits * targets, axis=1, keepdims=True)
         col_picked = jnp.sum(col_lse * targets, axis=1, keepdims=True)
         loss = 0.5 * (row_lse - picked) + 0.5 * (col_picked - picked)
-        loss_ref[0] = jnp.sum(loss) / replicas
+        loss_ref[...] = jnp.broadcast_to(
+            jnp.sum(loss, axis=0, keepdims=True) / replicas, loss_ref.shape
+        )
         if group > 1:
             settle(part_in, 4, group).wait_recv()
         d_std = jnp.sum(part_in[...], axis=0) * final_gain
@@ -547,6 +545,23 @@
         @pl.when(section == backward_relay)
         def _():
             backward_pass(slice(None)).wait_send()
+
+
+def deliver(next_ref, grad_ref, loss_ref, next_out, grad_out, loss_out, sem):
+    copies = [
+        pltpu.make_async_copy(source, target, sem.at[index])
+        for index, (source, target) in enumerate(
+            ((next_ref, next_out), (grad_ref, grad_out), (loss_ref, loss_out))
+        )
+    ]
+    for copy in copies:
+        copy.start()
+    for copy in copies:
+        copy.wait()
+
+
+def in_hbm(value):
+    return pltpu.with_memory_space_constraint(value, pltpu.HBM)
 
 
 def local(
@@ -571,13 +586,13 @@
     f32, bf16 = jnp.float32, jnp.bfloat16
     dma = pltpu.SemaphoreType.DMA
     vmem = pl.BlockSpec(memory_space=pltpu.VMEM)
-    whole = pl.BlockSpec(memory_space=pl.ANY)
+    hbm = pl.BlockSpec(memory_space=pltpu.HBM)
     big = pltpu.VMEM((tokens, width), bf16)
     next_raw, grad_raw, loss = pl.pallas_call(
         functools.partial(step_kernel, sections, replicas, group, unit),
-        out_shape=(big, big, jax.ShapeDtypeStruct((1,), f32)),
-        in_specs=[whole] * 9,
-        out_specs=(vmem, vmem, pl.BlockSpec(memory_space=pltpu.SMEM)),
+        out_shape=(big, big, pltpu.VMEM((1, 128), f32)),
+        in_specs=[hbm] * 8 + [pl.BlockSpec(memory_space=pltpu.SMEM)],
+        out_specs=(vmem, vmem, vmem),
         scratch_shapes=[
             big,
             big,
@@ -593,7 +608,6 @@
             pltpu.VMEM((1, width), f32),
             pltpu.VMEM((width,), f32),
             pltpu.VMEM((1, span), bf16),
-            pltpu.SMEM((1,), jnp.int32),
             pltpu.VMEM((sections * rows, shard), bf16),
             pltpu.VMEM((group, 1, width), f32),
             pltpu.VMEM((group, group, shard), f32),
@@ -603,7 +617,7 @@
             pltpu.VMEM((group, 1, width), f32),
             pltpu.VMEM((group, 1, width), f32),
             big,
-            dma((7,)),
+            dma((6,)),
             dma((chunks,)),
             dma((2,)),
             dma((3,)),
@@ -617,17 +631,30 @@
         ),
         name="tower_step",
     )(
-        activations[0, 0],
-        saved[0, 0],
-        cotangents[0, 0],
-        projection[0],
-        head_weight,
-        section_gain,
-        final_gain,
-        text_embed,
+        in_hbm(activations[0, 0]),
+        in_hbm(saved[0, 0]),
+        in_hbm(cotangents[0, 0]),
+        in_hbm(projection[0]),
+        in_hbm(head_weight),
+        in_hbm(section_gain),
+        in_hbm(final_gain),
+        in_hbm(text_embed),
         labels,
     )
-    return (next_raw[None, None], grad_raw[None, None], loss)
+    out = pltpu.HBM((tokens, width), bf16)
+    next_act, next_grad, mean_loss = pl.pallas_call(
+        deliver,
+        out_shape=(out, out, pltpu.HBM((1, 128), f32)),
+        in_specs=[vmem, vmem, vmem],
+        out_specs=(hbm, hbm, hbm),
+        scratch_shapes=[dma((3,))],
+        name="deliver",
+    )(
+        pltpu.with_memory_space_constraint(next_raw, pltpu.VMEM),
+        pltpu.with_memory_space_constraint(grad_raw, pltpu.VMEM),
+        pltpu.with_memory_space_constraint(loss, pltpu.VMEM),
+    )
+    return (next_act[None, None], next_grad[None, None], mean_loss[0, :1])
 
 
 def solution(mesh):

time: 53.8 us -> 41.4 us (0.77)
  local copies, waits for them, and re-layouts: 11.5 us -> 0 us
  between operations: 3.12 us -> 1.29 us
  Pallas kernels: 38.7 us -> 39.9 us
    unnamed x18 -> x0, local copies, waits for them, and re-layouts: 11.5 us -> none
    pallas_call x0 -> x1, Pallas kernels: none -> 1.27 us  [local(): pl.pallas_call(deliver, out_shape=(out, out, pltpu.HBM((1, 128), f32)), i...]
where the time goes in v2:
time: 41.4 us; the launch traced here: 41.2 us
  Pallas kernels  39.9 us (96%)
  between operations  1.29 us (3%)
    pallas_call x1, Pallas kernels, local(): pl.pallas_call(functools.partial(step_kernel, sections, replicas, group,...  38.6 us
    pallas_call x1, Pallas kernels, local(): pl.pallas_call(deliver, out_shape=(out, out, pltpu.HBM((1, 128), f32)), i...  1.27 us

profile of v2, /device:TPU:28, one launch (start us, length us, event | category | flops | bytes accessed | tf_op | source)
XLA Modules:
  0.0 41.2 jit_solution(17180714828000404915)
XLA Ops:
  1.3 38.6 %tower_step.1 = (bf16[257,1792]{1,0:T(8,128)(2,1)S(1)}, bf16[257,1792]{1,0:T(8,128)(2,1)S(1)}, f32[1,128]{1,0:T(1,128)S(1)}) custom-call(bf16[257,1792]{1,0:T(8,128)(2,1)} %bitcast.9, bf16[257,1792]{1,0:T(8,128)(2,1)} %bitcast.10, bf16[257,1792]{1,0:T(8,128)(2,1)} %bitcast.11, bf16[1792,1792]{1,0:T(8,128)(2,1)} %bitcast.8, bf16[448,1024]{1,0:T(8,128)(2,1)} %head_ref.1, ...), custom_call_target="tpu_custom_call" | custom-call | tf_op jit(solution)/shard_map/tower_step/pallas_call | solution.py:591
  39.9 1.3 %deliver.1 = (bf16[257,1792]{1,0:T(8,128)(2,1)}, bf16[257,1792]{1,0:T(8,128)(2,1)}, f32[1,128]{1,0:T(1,128)}) custom-call(bf16[257,1792]{1,0:T(8,128)(2,1)S(1)} %get-tuple-element.9.next_ref, bf16[257,1792]{1,0:T(8,128)(2,1)S(1)} %get-tuple-element.10.grad_ref, f32[1,128]{1,0:T(1,128)S(1)} %get-tuple-element.11.loss_ref), custom_call_target="tpu_custom_call" | custom-call | tf_op jit(solution)/shard_map/deliver/pallas_call | solution.py:645

commit v3 on v2

--- a/solution.py
+++ b/solution.py
@@ -11,7 +11,7 @@
 epsilon = 1e-06
 logit_scale = 100.0
 MESH = pl.DeviceIdType.MESH
-forward_share = 0.56
+forward_share = 0.58
 backward_share = 0.5
 
 
@@ -71,6 +71,7 @@
     relay_recv,
     small_send,
     small_recv,
+    ready,
 ):
     section, replica = lax.axis_index("section"), lax.axis_index("dp")
     last = sections - 1
@@ -118,7 +119,15 @@
             weight_ref.at[part, :], weight.at[part, :], weight_sem.at[index]
         )
 
-    load_act = pltpu.make_async_copy(act_ref, act, load_sem.at[0])
+    edge = int(tokens * forward_share) // 16 * 16
+    row_parts = (pl.ds(0, edge), pl.ds(edge, tokens - edge))
+
+    def load_act(part):
+        picked = row_parts[part]
+        return pltpu.make_async_copy(
+            act_ref.at[picked, :], act.at[picked, :], load_sem.at[(0, 6)[part]]
+        )
+
     load_saved = pltpu.make_async_copy(saved_ref, saved, load_sem.at[1])
     load_cot = pltpu.make_async_copy(cot_ref, cot, load_sem.at[2])
     load_scale = pltpu.make_async_copy(scale_ref, scale, load_sem.at[3])
@@ -127,21 +136,27 @@
 
     barrier = pltpu.get_barrier_semaphore()
 
-    def greet(axis, me, peers):
+    def greet(axis, me, peers, skip):
         def go(step, carry):
             peer = lax.rem(me + step, peers)
-            pl.semaphore_signal(barrier, inc=1, device_id={axis: peer}, device_id_type=MESH)
+
+            @pl.when(jnp.abs(me - peer) != skip)
+            def _():
+                pl.semaphore_signal(barrier, inc=1, device_id={axis: peer}, device_id_type=MESH)
+
             return carry
 
         lax.fori_loop(1, peers, go, 0)
 
-    greet("section", section, sections)
-    load_scale.start()
-
     @pl.when(section < last)
     def _():
-        load_act.start()
-        for index, (start, size) in enumerate(static_chunks):
+        load_act(0).start()
+        load_scale.start()
+        column_load(0, *static_chunks[0]).start()
+        load_act(1).start()
+
+    def other_loads():
+        for index, (start, size) in list(enumerate(static_chunks))[1:]:
             column_load(index, start, size).start()
 
         @pl.when(section > 0)
@@ -151,15 +166,22 @@
 
     @pl.when(section == last)
     def _():
-        greet("dp", replica, replicas)
+        load_saved.start()
         load_cot.start()
+        load_scale.start()
         for index, (start, size) in enumerate(static_chunks):
             row_load(index, start, size).start()
-            if index == 0:
-                load_saved.start()
-        load_act.start()
+        load_act(0).start()
+        load_act(1).start()
         load_text.start()
         load_gain.start()
+
+    direct = sections < 4
+    greet("section", section, sections, sections if direct else last)
+
+    @pl.when(section == last)
+    def _():
+        greet("dp", replica, replicas, replicas)
 
     my_columns = pl.ds(pl.multiple_of(slot * shard, shard), shard)
     away = pl.ds(0, last * rows)
@@ -200,12 +222,9 @@
     relays = sections >= 4
     forward_relay, backward_relay = middle + 1, middle - 2
 
-    def rows_at(share):
-        edge = int(tokens * share) // 16 * 16
-        return pl.ds(0, edge), pl.ds(edge, tokens - edge)
-
-    forward_near, forward_far = rows_at(forward_share)
-    backward_near, backward_far = rows_at(backward_share)
+    forward_near, forward_far = row_parts
+    bend = int(tokens * backward_share) // 16 * 16
+    backward_near, backward_far = pl.ds(0, bend), pl.ds(bend, tokens - bend)
 
     def forward_detour(index, columns_part):
         return move(
@@ -237,43 +256,109 @@
             relay, grad_ref, pass_send, backward_recv, middle - 1, (backward_far, columns_part)
         )
 
-    def send_piece(direct, detour, origin, near, index, columns_part):
+    def send_backward(index, columns_part):
         if not relays:
-            direct((slice(None), columns_part)).start()
+            backward_copy((slice(None), columns_part)).start()
             return
 
-        @pl.when(section == origin)
-        def _():
-            direct((near, columns_part)).start()
-            detour(index, columns_part).start()
-
-        @pl.when(section != origin)
-        def _():
-            direct((slice(None), columns_part)).start()
-
-    def forward():
-        load_act.wait()
-        values = act[...].astype(f32)
+        @pl.when(section == middle)
+        def _():
+            backward_copy((backward_near, columns_part)).start()
+            backward_detour(index, columns_part).start()
+
+        @pl.when(section != middle)
+        def _():
+            backward_copy((slice(None), columns_part)).start()
+
+    def send_forward(index, columns_part, part):
+        picked = row_parts[part]
+        if part == 0 or not relays:
+            forward_copy((picked, columns_part)).start()
+            return
+
+        @pl.when(section == middle - 1)
+        def _():
+            forward_detour(index, columns_part).start()
+
+        @pl.when(section != middle - 1)
+        def _():
+            forward_copy((picked, columns_part)).start()
+
+    def normalise(part):
+        picked = row_parts[part]
+        load_act(part).wait()
+        if part == 0:
+
+            @pl.when(section < last)
+            def _():
+                other_loads()
+
+        values = act[picked, :].astype(f32)
         centre, inverse = row_stats(values)
-        normed[...] = ((values - centre) * inverse * scale[...]).astype(bf16)
+        if part == 0:
+
+            @pl.when(section < last)
+            def _():
+                load_scale.wait()
+
+        normed[picked, :] = ((values - centre) * inverse * scale[...]).astype(bf16)
+
+    def mix(picked, columns_part):
+        mixed = jnp.dot(
+            normed[picked, :], weight[:, columns_part], preferred_element_type=f32
+        )
+        piece = (act[picked, columns_part].astype(f32) + mixed).astype(bf16)
+        block[picked, columns_part] = piece
+        return jnp.sum(piece.astype(f32), axis=0, keepdims=True)
+
+    def forward(before, between):
+        narrow = cut(*lead[0])
+        total = jnp.zeros((1, unit), f32)
+        for part in range(2):
+            normalise(part)
+            if part == 0:
+
+                @pl.when(section < last)
+                def _():
+                    column_load(0, *lead[0]).wait()
+
+            total = total + mix(row_parts[part], narrow)
+            if part == 0:
+                before()
+
+            @pl.when(section < last)
+            def _():
+                send_forward(0, narrow, part)
+
+        pooled[:, narrow] = total / tokens
+        between()
 
         def step(index, start, size):
-            part = cut(start, size)
+            columns_part = cut(start, size)
 
             @pl.when(section < last)
             def _():
                 column_load(index, start, size).wait()
 
-            mixed = jnp.dot(normed[...], weight[:, part], preferred_element_type=f32)
-            piece = (act[:, part].astype(f32) + mixed).astype(bf16)
-            block[:, part] = piece
-            pooled[:, part] = jnp.sum(piece.astype(f32), axis=0, keepdims=True) / tokens
+            pooled[:, columns_part] = mix(slice(None), columns_part) / tokens
 
             @pl.when(section < last)
             def _():
-                send_piece(forward_copy, forward_detour, middle - 1, forward_near, index, part)
-
-        each_chunk(step)
+                if relays:
+                    for part in range(2):
+                        send_forward(index, columns_part, part)
+                else:
+                    forward_copy((slice(None), columns_part)).start()
+
+        if pairs:
+
+            def go(index, carry):
+                step(index + 1, unit + index * wide, wide)
+                return carry
+
+            lax.fori_loop(0, pairs, go, 0)
+        for start, size in tail:
+            step(n_chunks - 1, start, size)
 
     def folded(values):
         total = values[:, 0:128]
@@ -285,6 +370,8 @@
         load_saved.wait()
         centre, inverse = row_stats(saved[...].astype(f32))
         load_cot.wait()
+        if wait_rows:
+            load_scale.wait()
         sum_slope[...] = jnp.zeros_like(sum_slope)
         sum_product[...] = jnp.zeros_like(sum_product)
 
@@ -319,7 +406,7 @@
                     - (saved[:, part].astype(f32) - centre) * factor
                 )
             ).astype(bf16)
-            send_piece(backward_copy, backward_detour, middle, backward_near, index, part)
+            send_backward(index, part)
             return carry
 
         lax.fori_loop(0, shards, emit, 0)
@@ -347,10 +434,8 @@
 
     @pl.when(section == last)
     def _():
-        load_scale.wait()
-
         def before_send():
-            pl.semaphore_wait(barrier, sections + replicas - 2)
+            pl.semaphore_wait(barrier, sections + replicas - (2 if direct else 3))
             own_head.start()
             load_text.wait()
             values = text[...].astype(f32)
@@ -361,13 +446,39 @@
 
         backward(True, before_send)
 
-    @pl.when(section < last)
-    def _():
-        pl.semaphore_wait(barrier, sections - 1)
-        head_copy().start()
-        load_scale.wait()
-
-    forward()
+    def enter_early():
+        @pl.when((section > (-1 if direct else 1)) & (section < last))
+        def _():
+            pl.semaphore_wait(barrier, sections - 1)
+            head_copy().start()
+
+    def enter_late():
+        if direct:
+            return
+
+        @pl.when(section == 0)
+        def _():
+            pl.semaphore_wait(barrier, sections - 2)
+
+        @pl.when(section == 1)
+        def _():
+            pl.semaphore_wait(barrier, sections - 1)
+            pl.semaphore_signal(ready, inc=1, device_id={"section": 0}, device_id_type=MESH)
+
+    def late_head():
+        if direct:
+            return
+
+        @pl.when(section == 0)
+        def _():
+            pl.semaphore_wait(ready, 1)
+
+        @pl.when(section < 2)
+        def _():
+            head_copy().start()
+
+    enter_early()
+    forward(enter_late, late_head)
 
     @pl.when((section > 0) & (section < last))
     def _():
@@ -617,7 +728,7 @@
             pltpu.VMEM((group, 1, width), f32),
             pltpu.VMEM((group, 1, width), f32),
             big,
-            dma((6,)),
+            dma((7,)),
             dma((chunks,)),
             dma((2,)),
             dma((3,)),
@@ -625,6 +736,7 @@
             dma((shards,)),
             dma((5,)),
             dma((5,)),
+            pltpu.SemaphoreType.REGULAR,
         ],
         compiler_params=pltpu.CompilerParams(
             collective_id=0, has_side_effects=True, vmem_limit_bytes=40 * 1024 * 1024

time: 41.4 us -> 40 us (0.966)
  Pallas kernels: 39.9 us -> 38.3 us
    pallas_call x1, Pallas kernels: 38.6 us -> 37.1 us  [local(): pl.pallas_call(functools.partial(step_kernel, sections, replicas, group,...]
where the time goes in v3:
time: 40 us; the launch traced here: 39.6 us
  Pallas kernels  38.3 us (96%)
  between operations  1.29 us (3%)
    pallas_call x1, Pallas kernels, local(): pl.pallas_call(functools.partial(step_kernel, sections, replicas, group,...  37.1 us
    pallas_call x1, Pallas kernels, local(): pl.pallas_call(deliver, out_shape=(out, out, pltpu.HBM((1, 128), f32)), i...  1.27 us

profile of v3, /device:TPU:28, one launch (start us, length us, event | category | flops | bytes accessed | tf_op | source)
XLA Modules:
  0.0 39.6 jit_solution(13201328474916423005)
XLA Ops:
  1.3 37.1 %tower_step.1 = (bf16[257,1792]{1,0:T(8,128)(2,1)S(1)}, bf16[257,1792]{1,0:T(8,128)(2,1)S(1)}, f32[1,128]{1,0:T(1,128)S(1)}) custom-call(bf16[257,1792]{1,0:T(8,128)(2,1)} %bitcast.9, bf16[257,1792]{1,0:T(8,128)(2,1)} %bitcast.10, bf16[257,1792]{1,0:T(8,128)(2,1)} %bitcast.11, bf16[1792,1792]{1,0:T(8,128)(2,1)} %bitcast.8, bf16[448,1024]{1,0:T(8,128)(2,1)} %head_ref.1, ...), custom_call_target="tpu_custom_call" | custom-call | tf_op jit(solution)/shard_map/tower_step/pallas_call | solution.py:702
  38.4 1.3 %deliver.1 = (bf16[257,1792]{1,0:T(8,128)(2,1)}, bf16[257,1792]{1,0:T(8,128)(2,1)}, f32[1,128]{1,0:T(1,128)}) custom-call(bf16[257,1792]{1,0:T(8,128)(2,1)S(1)} %get-tuple-element.9.next_ref, bf16[257,1792]{1,0:T(8,128)(2,1)S(1)} %get-tuple-element.10.grad_ref, f32[1,128]{1,0:T(1,128)S(1)} %get-tuple-element.11.loss_ref), custom_call_target="tpu_custom_call" | custom-call | tf_op jit(solution)/shard_map/deliver/pallas_call | solution.py:757

commit v4 on v3

--- a/solution.py
+++ b/solution.py
@@ -11,7 +11,8 @@
 epsilon = 1e-06
 logit_scale = 100.0
 MESH = pl.DeviceIdType.MESH
-forward_share = 0.58
+narrow_share = 0.60
+wide_share = 0.60
 backward_share = 0.5
 
 
@@ -119,11 +120,14 @@
             weight_ref.at[part, :], weight.at[part, :], weight_sem.at[index]
         )
 
-    edge = int(tokens * forward_share) // 16 * 16
-    row_parts = (pl.ds(0, edge), pl.ds(edge, tokens - edge))
+    def rows_at(share):
+        edge = int(tokens * share) // 8 * 8
+        return pl.ds(0, edge), pl.ds(edge, tokens - edge)
+
+    narrow_rows, wide_rows = rows_at(narrow_share), rows_at(wide_share)
 
     def load_act(part):
-        picked = row_parts[part]
+        picked = narrow_rows[part]
         return pltpu.make_async_copy(
             act_ref.at[picked, :], act.at[picked, :], load_sem.at[(0, 6)[part]]
         )
@@ -134,6 +138,12 @@
     load_gain = pltpu.make_async_copy(gain_ref, gain, load_sem.at[4])
     load_text = pltpu.make_async_copy(text_ref, text, load_sem.at[5])
 
+    my_columns = pl.ds(pl.multiple_of(slot * shard, shard), shard)
+    own_rows = pl.ds(pl.multiple_of(section * rows, rows), rows)
+    own_head = pltpu.make_async_copy(
+        head_ref.at[:, my_columns], heads.at[own_rows, :], head_sem.at[2]
+    )
+
     barrier = pltpu.get_barrier_semaphore()
 
     def greet(axis, me, peers, skip):
@@ -153,6 +163,7 @@
         load_act(0).start()
         load_scale.start()
         column_load(0, *static_chunks[0]).start()
+        own_head.start()
         load_act(1).start()
 
     def other_loads():
@@ -175,6 +186,7 @@
         load_act(1).start()
         load_text.start()
         load_gain.start()
+        own_head.start()
 
     direct = sections < 4
     greet("section", section, sections, sections if direct else last)
@@ -183,13 +195,12 @@
     def _():
         greet("dp", replica, replicas, replicas)
 
-    my_columns = pl.ds(pl.multiple_of(slot * shard, shard), shard)
     away = pl.ds(0, last * rows)
 
     def head_copy():
         return pltpu.make_async_remote_copy(
-            head_ref.at[:, my_columns],
-            heads.at[pl.ds(pl.multiple_of(section * rows, rows), rows), :],
+            heads.at[own_rows, :],
+            heads.at[own_rows, :],
             head_sem.at[0],
             head_sem.at[1],
             {"section": last},
@@ -199,9 +210,10 @@
     head_arrival = pltpu.make_async_remote_copy(
         heads.at[away, :], heads.at[away, :], head_sem.at[0], head_sem.at[1], {"section": 0}, MESH
     )
-    own_head = pltpu.make_async_copy(
-        head_ref.at[:, my_columns], heads.at[pl.ds(last * rows, rows), :], head_sem.at[0]
-    )
+
+    def send_head():
+        own_head.wait()
+        head_copy().start()
 
     everything = (slice(None), slice(None))
     forward_send, backward_send, pass_send = bulk_send.at[0], bulk_send.at[1], bulk_send.at[2]
@@ -222,9 +234,10 @@
     relays = sections >= 4
     forward_relay, backward_relay = middle + 1, middle - 2
 
-    forward_near, forward_far = row_parts
-    bend = int(tokens * backward_share) // 16 * 16
-    backward_near, backward_far = pl.ds(0, bend), pl.ds(bend, tokens - bend)
+    backward_near, backward_far = rows_at(backward_share)
+
+    def forward_rows(index):
+        return narrow_rows if isinstance(index, int) and index == 0 else wide_rows
 
     def forward_detour(index, columns_part):
         return move(
@@ -233,7 +246,7 @@
             forward_send,
             relay_recv.at[index],
             forward_relay,
-            (forward_far, columns_part),
+            (forward_rows(index)[1], columns_part),
         )
 
     def backward_detour(index, columns_part):
@@ -246,9 +259,14 @@
             (backward_far, columns_part),
         )
 
-    def forward_pass(columns_part):
+    def forward_pass(index, columns_part):
         return move(
-            relay, next_ref, pass_send, forward_recv, middle, (forward_far, columns_part)
+            relay,
+            next_ref,
+            pass_send,
+            forward_recv,
+            middle,
+            (forward_rows(index)[1], columns_part),
         )
 
     def backward_pass(columns_part):
@@ -270,8 +288,21 @@
         def _():
             backward_copy((slice(None), columns_part)).start()
 
+    held = relays and n_chunks > 1 and middle > 1
+
+    def send_held():
+        part = cut(*static_chunks[-1])
+        forward_copy((forward_rows(1)[0], part)).start()
+
     def send_forward(index, columns_part, part):
-        picked = row_parts[part]
+        picked = forward_rows(index)[part]
+        if part == 0 and held and not (isinstance(index, int) and index == 0):
+
+            @pl.when((section != middle - 1) | (index != n_chunks - 1))
+            def _():
+                forward_copy((picked, columns_part)).start()
+
+            return
         if part == 0 or not relays:
             forward_copy((picked, columns_part)).start()
             return
@@ -285,7 +316,7 @@
             forward_copy((picked, columns_part)).start()
 
     def normalise(part):
-        picked = row_parts[part]
+        picked = narrow_rows[part]
         load_act(part).wait()
         if part == 0:
 
@@ -322,7 +353,7 @@
                 def _():
                     column_load(0, *lead[0]).wait()
 
-            total = total + mix(row_parts[part], narrow)
+            total = total + mix(narrow_rows[part], narrow)
             if part == 0:
                 before()
 
@@ -365,6 +396,10 @@
         for start in range(128, values.shape[-1], 128):
             total = total + values[:, start : start + 128]
         return total
+
+    def relay_forward(index, part):
+        forward_detour(index, part).wait_recv()
+        forward_pass(index, part).start()
 
     def backward(wait_rows, before_send):
         load_saved.wait()
@@ -390,7 +425,11 @@
             sum_slope[...] += folded(piece)
             sum_product[...] += folded(piece * (saved[:, part].astype(f32) - centre))
 
-        each_chunk(step)
+        if wait_rows:
+            for index, (start, size) in enumerate(static_chunks):
+                step(index, start, size)
+        else:
+            each_chunk(step)
         mean_slope = jnp.sum(sum_slope[...], axis=-1, keepdims=True) / width
         mean_product = inverse * (jnp.sum(sum_product[...], axis=-1, keepdims=True) / width)
         offset = inverse * mean_slope
@@ -436,7 +475,6 @@
     def _():
         def before_send():
             pl.semaphore_wait(barrier, sections + replicas - (2 if direct else 3))
-            own_head.start()
             load_text.wait()
             values = text[...].astype(f32)
             text_inv = lax.rsqrt(jnp.sum(values * values, axis=-1, keepdims=True) + epsilon)
@@ -450,7 +488,7 @@
         @pl.when((section > (-1 if direct else 1)) & (section < last))
         def _():
             pl.semaphore_wait(barrier, sections - 1)
-            head_copy().start()
+            send_head()
 
     def enter_late():
         if direct:
@@ -475,7 +513,7 @@
 
         @pl.when(section < 2)
         def _():
-            head_copy().start()
+            send_head()
 
     enter_early()
     forward(enter_late, late_head)
@@ -483,6 +521,11 @@
     @pl.when((section > 0) & (section < last))
     def _():
         backward(False, lambda: None)
+        if held:
+
+            @pl.when(section == middle - 1)
+            def _():
+                send_held()
 
     @pl.when(section == 0)
     def _():
@@ -492,13 +535,9 @@
     def _():
         loss_ref[...] = jnp.zeros_like(loss_ref)
 
-    def forward_relays():
-        def go(index, start, size):
-            part = cut(start, size)
-            forward_detour(index, part).wait_recv()
-            forward_pass(part).start()
-
-        each_chunk(go)
+    def forward_relays(skip):
+        for index, (start, size) in list(enumerate(static_chunks))[skip:]:
+            relay_forward(index, cut(start, size))
 
     def backward_relays():
         def go(index, carry):
@@ -519,7 +558,7 @@
 
             @pl.when(section == forward_relay)
             def _():
-                forward_relays()
+                forward_relays(0)
 
     @pl.when(section == last)
     def _():
@@ -548,7 +587,7 @@
         if group > 1:
             settle(columns, 2, group).wait_recv()
         if relays and forward_relay == last:
-            forward_relays()
+            forward_relays(0)
         embedding = jnp.concatenate([columns[index] for index in range(group)], axis=1)
         image_inv = lax.rsqrt(jnp.sum(embedding * embedding, axis=-1, keepdims=True) + epsilon)
         image_unit = embedding * image_inv
@@ -651,7 +690,8 @@
 
         @pl.when(section == forward_relay)
         def _():
-            forward_pass(slice(None)).wait_send()
+            for index, (start, size) in enumerate(static_chunks):
+                forward_pass(index, cut(start, size)).wait_send()
 
         @pl.when(section == backward_relay)
         def _():
@@ -730,7 +770,7 @@
             big,
             dma((7,)),
             dma((chunks,)),
-            dma((2,)),
+            dma((3,)),
             dma((3,)),
             dma((2,)),
             dma((shards,)),

time: 40 us -> 39.4 us (0.985)
  Pallas kernels: 38.3 us -> 37.7 us
    pallas_call x1, Pallas kernels: 37.1 us -> 36.5 us  [local(): pl.pallas_call(functools.partial(step_kernel, sections, replicas, group,...]
where the time goes in v4:
time: 39.4 us; the launch traced here: 39 us
  Pallas kernels  37.7 us (96%)
  between operations  1.29 us (3%)
    pallas_call x1, Pallas kernels, local(): pl.pallas_call(functools.partial(step_kernel, sections, replicas, group,...  36.5 us
    pallas_call x1, Pallas kernels, local(): pl.pallas_call(deliver, out_shape=(out, out, pltpu.HBM((1, 128), f32)), i...  1.27 us

profile of v4, /device:TPU:28, one launch (start us, length us, event | category | flops | bytes accessed | tf_op | source)
XLA Modules:
  0.0 39.0 jit_solution(7171579402386588019)
XLA Ops:
  1.3 36.5 %tower_step.1 = (bf16[257,1792]{1,0:T(8,128)(2,1)S(1)}, bf16[257,1792]{1,0:T(8,128)(2,1)S(1)}, f32[1,128]{1,0:T(1,128)S(1)}) custom-call(bf16[257,1792]{1,0:T(8,128)(2,1)} %bitcast.9, bf16[257,1792]{1,0:T(8,128)(2,1)} %bitcast.10, bf16[257,1792]{1,0:T(8,128)(2,1)} %bitcast.11, bf16[1792,1792]{1,0:T(8,128)(2,1)} %bitcast.8, bf16[448,1024]{1,0:T(8,128)(2,1)} %head_ref.1, ...), custom_call_target="tpu_custom_call" | custom-call | tf_op jit(solution)/shard_map/tower_step/pallas_call | solution.py:742
  37.8 1.3 %deliver.1 = (bf16[257,1792]{1,0:T(8,128)(2,1)}, bf16[257,1792]{1,0:T(8,128)(2,1)}, f32[1,128]{1,0:T(1,128)}) custom-call(bf16[257,1792]{1,0:T(8,128)(2,1)S(1)} %get-tuple-element.9.next_ref, bf16[257,1792]{1,0:T(8,128)(2,1)S(1)} %get-tuple-element.10.grad_ref, f32[1,128]{1,0:T(1,128)S(1)} %get-tuple-element.11.loss_ref), custom_call_target="tpu_custom_call" | custom-call | tf_op jit(solution)/shard_map/deliver/pallas_call | solution.py:797

commit v5 on v4

--- a/solution.py
+++ b/solution.py
@@ -11,7 +11,7 @@
 epsilon = 1e-06
 logit_scale = 100.0
 MESH = pl.DeviceIdType.MESH
-narrow_share = 0.60
+narrow_share = 0.56
 wide_share = 0.60
 backward_share = 0.5
 
@@ -83,6 +83,8 @@
     slot = lax.rem(replica, group)
     first = replica - slot
     shard = span // group
+    middle = sections // 2
+    relays = sections >= 4
     f32, bf16 = jnp.float32, jnp.bfloat16
     wide = 2 * unit
     lead = [(0, unit)]
@@ -129,19 +131,19 @@
     def load_act(part):
         picked = narrow_rows[part]
         return pltpu.make_async_copy(
-            act_ref.at[picked, :], act.at[picked, :], load_sem.at[(0, 6)[part]]
-        )
-
-    load_saved = pltpu.make_async_copy(saved_ref, saved, load_sem.at[1])
+            act_ref.at[picked, :], act.at[picked, :], load_sem.at[(4, 1)[part]]
+        )
+
+    load_saved = pltpu.make_async_copy(saved_ref, saved, load_sem.at[0])
     load_cot = pltpu.make_async_copy(cot_ref, cot, load_sem.at[2])
     load_scale = pltpu.make_async_copy(scale_ref, scale, load_sem.at[3])
-    load_gain = pltpu.make_async_copy(gain_ref, gain, load_sem.at[4])
-    load_text = pltpu.make_async_copy(text_ref, text, load_sem.at[5])
+    load_gain = pltpu.make_async_copy(gain_ref, gain, load_sem.at[2])
+    load_text = pltpu.make_async_copy(text_ref, text, load_sem.at[0])
 
     my_columns = pl.ds(pl.multiple_of(slot * shard, shard), shard)
     own_rows = pl.ds(pl.multiple_of(section * rows, rows), rows)
     own_head = pltpu.make_async_copy(
-        head_ref.at[:, my_columns], heads.at[own_rows, :], head_sem.at[2]
+        head_ref.at[:, my_columns], heads.at[own_rows, :], head_sem.at[0]
     )
 
     barrier = pltpu.get_barrier_semaphore()
@@ -163,6 +165,23 @@
         load_act(0).start()
         load_scale.start()
         column_load(0, *static_chunks[0]).start()
+
+    @pl.when(section == last)
+    def _():
+        load_saved.start()
+        load_cot.start()
+        load_scale.start()
+        row_load(0, *static_chunks[0]).start()
+
+    chain = relays
+    greet("section", section, sections, last if chain else sections)
+
+    @pl.when(section == last)
+    def _():
+        greet("dp", replica, replicas, replicas)
+
+    @pl.when(section < last)
+    def _():
         own_head.start()
         load_act(1).start()
 
@@ -177,23 +196,11 @@
 
     @pl.when(section == last)
     def _():
-        load_saved.start()
-        load_cot.start()
-        load_scale.start()
-        for index, (start, size) in enumerate(static_chunks):
+        for index, (start, size) in list(enumerate(static_chunks))[1:]:
             row_load(index, start, size).start()
         load_act(0).start()
         load_act(1).start()
-        load_text.start()
-        load_gain.start()
         own_head.start()
-
-    direct = sections < 4
-    greet("section", section, sections, sections if direct else last)
-
-    @pl.when(section == last)
-    def _():
-        greet("dp", replica, replicas, replicas)
 
     away = pl.ds(0, last * rows)
 
@@ -230,8 +237,6 @@
     def backward_copy(part):
         return move(d_input, grad_ref, backward_send, backward_recv, section - 1, part)
 
-    middle = sections // 2
-    relays = sections >= 4
     forward_relay, backward_relay = middle + 1, middle - 2
 
     backward_near, backward_far = rows_at(backward_share)
@@ -406,6 +411,8 @@
         centre, inverse = row_stats(saved[...].astype(f32))
         load_cot.wait()
         if wait_rows:
+            load_text.start()
+            load_gain.start()
             load_scale.wait()
         sum_slope[...] = jnp.zeros_like(sum_slope)
         sum_product[...] = jnp.zeros_like(sum_product)
@@ -436,8 +443,8 @@
         factor = inverse * inverse * mean_product
         before_send()
 
-        def emit(index, carry):
-            part = cut(index * unit, unit)
+        def emit(index, start, size):
+            part = cut(start, size)
             d_input[:, part] = (
                 cot[:, part].astype(f32)
                 + (
@@ -446,9 +453,8 @@
                 )
             ).astype(bf16)
             send_backward(index, part)
-            return carry
-
-        lax.fori_loop(0, shards, emit, 0)
+
+        each_chunk(emit)
 
     def exchange(slots, pair, axis, me, base, peers):
         def go(step, carry):
@@ -474,7 +480,7 @@
     @pl.when(section == last)
     def _():
         def before_send():
-            pl.semaphore_wait(barrier, sections + replicas - (2 if direct else 3))
+            pl.semaphore_wait(barrier, sections + replicas - (3 if chain else 2))
             load_text.wait()
             values = text[...].astype(f32)
             text_inv = lax.rsqrt(jnp.sum(values * values, axis=-1, keepdims=True) + epsilon)
@@ -484,38 +490,45 @@
 
         backward(True, before_send)
 
-    def enter_early():
-        @pl.when((section > (-1 if direct else 1)) & (section < last))
+    def tell_first():
+        @pl.when(section == 1)
+        def _():
+            pl.semaphore_signal(ready, inc=1, device_id={"section": 0}, device_id_type=MESH)
+
+    late = (section == 0) | (section == middle - 1) if chain else section < 0
+
+    @pl.when(jnp.logical_not(late) & (section < last))
+    def _():
+        pl.semaphore_wait(barrier, sections - 1)
+        if chain:
+            tell_first()
+        send_head()
+
+    def enter_late():
+        if not chain:
+            return
+
+        @pl.when(section == 0)
+        def _():
+            pl.semaphore_wait(barrier, sections - 2)
+
+        @pl.when(section == middle - 1)
         def _():
             pl.semaphore_wait(barrier, sections - 1)
+            tell_first()
+
+    def late_head():
+        if not chain:
+            return
+
+        @pl.when(section == 0)
+        def _():
+            pl.semaphore_wait(ready, 1)
+
+        @pl.when(late)
+        def _():
             send_head()
 
-    def enter_late():
-        if direct:
-            return
-
-        @pl.when(section == 0)
-        def _():
-            pl.semaphore_wait(barrier, sections - 2)
-
-        @pl.when(section == 1)
-        def _():
-            pl.semaphore_wait(barrier, sections - 1)
-            pl.semaphore_signal(ready, inc=1, device_id={"section": 0}, device_id_type=MESH)
-
-    def late_head():
-        if direct:
-            return
-
-        @pl.when(section == 0)
-        def _():
-            pl.semaphore_wait(ready, 1)
-
-        @pl.when(section < 2)
-        def _():
-            send_head()
-
-    enter_early()
     forward(enter_late, late_head)
 
     @pl.when((section > 0) & (section < last))
@@ -540,13 +553,12 @@
             relay_forward(index, cut(start, size))
 
     def backward_relays():
-        def go(index, carry):
-            part = cut(index * unit, unit)
+        def go(index, start, size):
+            part = cut(start, size)
             backward_detour(index, part).wait_recv()
             backward_pass(part).start()
-            return carry
-
-        lax.fori_loop(0, shards, go, 0)
+
+        each_chunk(go)
 
     if relays:
 
@@ -598,8 +610,8 @@
             images[replica] = jnp.sum(
                 jnp.where(member == slot, image_unit, 0.0), axis=0, keepdims=True
             )
-            exchange(images, 3, "dp", replica, 0, replicas)
-            settle(images, 3, replicas).wait_recv()
+            exchange(images, 4, "dp", replica, 0, replicas)
+            settle(images, 4, replicas).wait_recv()
             all_image = images[:, 0, :]
         logits = logit_scale * lax.dot_general(
             all_image,
@@ -643,8 +655,8 @@
             pltpu.make_async_remote_copy(
                 part_out.at[peer],
                 part_in.at[slot],
-                small_send.at[4],
-                small_recv.at[4],
+                small_send.at[3],
+                small_recv.at[3],
                 {"dp": first + peer},
                 MESH,
             ).start()
@@ -659,7 +671,7 @@
             jnp.sum(loss, axis=0, keepdims=True) / replicas, loss_ref.shape
         )
         if group > 1:
-            settle(part_in, 4, group).wait_recv()
+            settle(part_in, 3, group).wait_recv()
         d_std = jnp.sum(part_in[...], axis=0) * final_gain
         d_pooled = pooled_inv * (
             d_std
@@ -671,9 +683,9 @@
         if group > 1:
             settle(feats, 1, group).wait_send()
             settle(columns, 2, group).wait_send()
-            settle(part_out, 4, group).wait_send()
+            settle(part_out, 3, group).wait_send()
         if replicas != group:
-            settle(images, 3, replicas).wait_send()
+            settle(images, 4, replicas).wait_send()
 
     @pl.when(section < last)
     def _():
@@ -734,6 +746,7 @@
     unit = 256 if width % 256 == 0 else 128
     shards = width // unit
     chunks = 1 + (shards - 1) // 2 + (shards - 1) % 2
+    smalls = 4 if replicas == group else 5
     f32, bf16 = jnp.float32, jnp.bfloat16
     dma = pltpu.SemaphoreType.DMA
     vmem = pl.BlockSpec(memory_space=pltpu.VMEM)
@@ -768,14 +781,14 @@
             pltpu.VMEM((group, 1, width), f32),
             pltpu.VMEM((group, 1, width), f32),
             big,
-            dma((7,)),
+            dma((5,)),
             dma((chunks,)),
-            dma((3,)),
+            dma((2,)),
             dma((3,)),
             dma((2,)),
-            dma((shards,)),
-            dma((5,)),
-            dma((5,)),
+            dma((chunks,)),
+            dma((smalls,)),
+            dma((smalls,)),
             pltpu.SemaphoreType.REGULAR,
         ],
         compiler_params=pltpu.CompilerParams(

time: 39.4 us -> 39.3 us (level)
  no operation moved by 1% of the time
where the time goes in v5:
time: 39.3 us; the launch traced here: 39 us
  Pallas kernels  37.7 us (96%)
  between operations  1.29 us (3%)
    pallas_call x1, Pallas kernels, local(): pl.pallas_call(functools.partial(step_kernel, sections, replicas, group,...  36.4 us
    pallas_call x1, Pallas kernels, local(): pl.pallas_call(deliver, out_shape=(out, out, pltpu.HBM((1, 128), f32)), i...  1.27 us

profile of v5, /device:TPU:28, one launch (start us, length us, event | category | flops | bytes accessed | tf_op | source)
XLA Modules:
  0.0 39.0 jit_solution(17656773430934464512)
XLA Ops:
  1.3 36.4 %tower_step.1 = (bf16[257,1792]{1,0:T(8,128)(2,1)S(1)}, bf16[257,1792]{1,0:T(8,128)(2,1)S(1)}, f32[1,128]{1,0:T(1,128)S(1)}) custom-call(bf16[257,1792]{1,0:T(8,128)(2,1)} %bitcast.9, bf16[257,1792]{1,0:T(8,128)(2,1)} %bitcast.10, bf16[257,1792]{1,0:T(8,128)(2,1)} %bitcast.11, bf16[1792,1792]{1,0:T(8,128)(2,1)} %bitcast.8, bf16[448,1024]{1,0:T(8,128)(2,1)} %head_ref.1, ...), custom_call_target="tpu_custom_call" | custom-call | tf_op jit(solution)/shard_map/tower_step/pallas_call | solution.py:755
  37.7 1.3 %deliver.1 = (bf16[257,1792]{1,0:T(8,128)(2,1)}, bf16[257,1792]{1,0:T(8,128)(2,1)}, f32[1,128]{1,0:T(1,128)}) custom-call(bf16[257,1792]{1,0:T(8,128)(2,1)S(1)} %get-tuple-element.9.next_ref, bf16[257,1792]{1,0:T(8,128)(2,1)S(1)} %get-tuple-element.10.grad_ref, f32[1,128]{1,0:T(1,128)S(1)} %get-tuple-element.11.loss_ref), custom_call_target="tpu_custom_call" | custom-call | tf_op jit(solution)/shard_map/deliver/pallas_call | solution.py:810

commit v6 on v5

--- a/solution.py
+++ b/solution.py
@@ -13,7 +13,7 @@
 MESH = pl.DeviceIdType.MESH
 narrow_share = 0.56
 wide_share = 0.60
-backward_share = 0.5
+backward_share = 0.53
 
 
 def row_stats(values):
@@ -293,17 +293,27 @@
         def _():
             backward_copy((slice(None), columns_part)).start()
 
-    held = relays and n_chunks > 1 and middle > 1
+    held = relays and n_chunks > 1
+
+    def keeps(index):
+        return ((section == middle - 1) | (section == middle)) & (index == n_chunks - 1)
 
     def send_held():
         part = cut(*static_chunks[-1])
-        forward_copy((forward_rows(1)[0], part)).start()
+
+        @pl.when(section == middle - 1)
+        def _():
+            forward_copy((forward_rows(1)[0], part)).start()
+
+        @pl.when(section == middle)
+        def _():
+            forward_copy((slice(None), part)).start()
 
     def send_forward(index, columns_part, part):
         picked = forward_rows(index)[part]
         if part == 0 and held and not (isinstance(index, int) and index == 0):
 
-            @pl.when((section != middle - 1) | (index != n_chunks - 1))
+            @pl.when(jnp.logical_not(keeps(index)))
             def _():
                 forward_copy((picked, columns_part)).start()
 
@@ -316,7 +326,11 @@
         def _():
             forward_detour(index, columns_part).start()
 
-        @pl.when(section != middle - 1)
+        stays = section != middle - 1
+        if held and not (isinstance(index, int) and index == 0):
+            stays = stays & jnp.logical_not(keeps(index))
+
+        @pl.when(stays)
         def _():
             forward_copy((picked, columns_part)).start()
 
@@ -536,9 +550,7 @@
         backward(False, lambda: None)
         if held:
 
-            @pl.when(section == middle - 1)
-            def _():
-                send_held()
+            send_held()
 
     @pl.when(section == 0)
     def _():

time: 39.3 us -> 39.2 us (level)
  no operation moved by 1% of the time
where the time goes in v6:
time: 39.2 us; the launch traced here: 39 us
  Pallas kernels  37.7 us (96%)
  between operations  1.29 us (3%)
    pallas_call x1, Pallas kernels, local(): pl.pallas_call(functools.partial(step_kernel, sections, replicas, group,...  36.4 us
    pallas_call x1, Pallas kernels, local(): pl.pallas_call(deliver, out_shape=(out, out, pltpu.HBM((1, 128), f32)), i...  1.27 us

profile of v6, /device:TPU:28, one launch (start us, length us, event | category | flops | bytes accessed | tf_op | source)
XLA Modules:
  0.0 39.0 jit_solution(7564471099781799005)
XLA Ops:
  1.3 36.4 %tower_step.1 = (bf16[257,1792]{1,0:T(8,128)(2,1)S(1)}, bf16[257,1792]{1,0:T(8,128)(2,1)S(1)}, f32[1,128]{1,0:T(1,128)S(1)}) custom-call(bf16[257,1792]{1,0:T(8,128)(2,1)} %bitcast.9, bf16[257,1792]{1,0:T(8,128)(2,1)} %bitcast.10, bf16[257,1792]{1,0:T(8,128)(2,1)} %bitcast.11, bf16[1792,1792]{1,0:T(8,128)(2,1)} %bitcast.8, bf16[448,1024]{1,0:T(8,128)(2,1)} %head_ref.1, ...), custom_call_target="tpu_custom_call" | custom-call | tf_op jit(solution)/shard_map/tower_step/pallas_call | solution.py:767
  37.7 1.3 %deliver.1 = (bf16[257,1792]{1,0:T(8,128)(2,1)}, bf16[257,1792]{1,0:T(8,128)(2,1)}, f32[1,128]{1,0:T(1,128)}) custom-call(bf16[257,1792]{1,0:T(8,128)(2,1)S(1)} %get-tuple-element.9.next_ref, bf16[257,1792]{1,0:T(8,128)(2,1)S(1)} %get-tuple-element.10.grad_ref, f32[1,128]{1,0:T(1,128)S(1)} %get-tuple-element.11.loss_ref), custom_call_target="tpu_custom_call" | custom-call | tf_op jit(solution)/shard_map/deliver/pallas_call | solution.py:822

commit v7 on v6

--- a/solution.py
+++ b/solution.py
@@ -11,7 +11,7 @@
 epsilon = 1e-06
 logit_scale = 100.0
 MESH = pl.DeviceIdType.MESH
-narrow_share = 0.56
+narrow_share = 0.63
 wide_share = 0.60
 backward_share = 0.53
 
@@ -198,9 +198,6 @@
     def _():
         for index, (start, size) in list(enumerate(static_chunks))[1:]:
             row_load(index, start, size).start()
-        load_act(0).start()
-        load_act(1).start()
-        own_head.start()
 
     away = pl.ds(0, last * rows)
 
@@ -449,6 +446,10 @@
         if wait_rows:
             for index, (start, size) in enumerate(static_chunks):
                 step(index, start, size)
+                if index == min(1, n_chunks - 1):
+                    load_act(0).start()
+                    load_act(1).start()
+                    own_head.start()
         else:
             each_chunk(step)
         mean_slope = jnp.sum(sum_slope[...], axis=-1, keepdims=True) / width

time: 39.2 us -> 39.1 us (level)
  no operation moved by 1% of the time
where the time goes in v7:
time: 39.1 us; the launch traced here: 38.9 us
  Pallas kernels  37.6 us (96%)
  between operations  1.29 us (3%)
    pallas_call x1, Pallas kernels, local(): pl.pallas_call(functools.partial(step_kernel, sections, replicas, group,...  36.4 us
    pallas_call x1, Pallas kernels, local(): pl.pallas_call(deliver, out_shape=(out, out, pltpu.HBM((1, 128), f32)), i...  1.27 us

profile of v7, /device:TPU:28, one launch (start us, length us, event | category | flops | bytes accessed | tf_op | source)
XLA Modules:
  0.0 38.9 jit_solution(16822334102609101649)
XLA Ops:
  1.3 36.4 %tower_step.1 = (bf16[257,1792]{1,0:T(8,128)(2,1)S(1)}, bf16[257,1792]{1,0:T(8,128)(2,1)S(1)}, f32[1,128]{1,0:T(1,128)S(1)}) custom-call(bf16[257,1792]{1,0:T(8,128)(2,1)} %bitcast.9, bf16[257,1792]{1,0:T(8,128)(2,1)} %bitcast.10, bf16[257,1792]{1,0:T(8,128)(2,1)} %bitcast.11, bf16[1792,1792]{1,0:T(8,128)(2,1)} %bitcast.8, bf16[448,1024]{1,0:T(8,128)(2,1)} %head_ref.1, ...), custom_call_target="tpu_custom_call" | custom-call | tf_op jit(solution)/shard_map/tower_step/pallas_call | solution.py:768
  37.7 1.3 %deliver.1 = (bf16[257,1792]{1,0:T(8,128)(2,1)}, bf16[257,1792]{1,0:T(8,128)(2,1)}, f32[1,128]{1,0:T(1,128)}) custom-call(bf16[257,1792]{1,0:T(8,128)(2,1)S(1)} %get-tuple-element.9.next_ref, bf16[257,1792]{1,0:T(8,128)(2,1)S(1)} %get-tuple-element.10.grad_ref, f32[1,128]{1,0:T(1,128)S(1)} %get-tuple-element.11.loss_ref), custom_call_target="tpu_custom_call" | custom-call | tf_op jit(solution)/shard_map/deliver/pallas_call | solution.py:823
